TPU v7x, 128 devices: a whole 4x4x4 slice. The times are simulated.
128 devices in a mesh: dom: 16 (over x, y), harm: 8 (over z, core).
Axes of the slice: x: 4, y: 4, z: 4, core: 2. Of those that a mesh axis runs over, the one named last changes fastest.
Arguments:
- basis: float32 [20, 2, 256, 32768], P(None, None, 'harm', 'dom'), may hold values from -200 to 200, as said below
- coeffs: float32 [20], replicated, may hold values from -4 to 4
- conductance_tiles: float32 [256, 6, 128, 128], P('dom'), may hold values from -0.21875 to 0.21875
- tile_cols: int32 [256, 6], P('dom'), may hold values from 0 to 31, as said below
- self_cond: float32 [32768], P('dom'), may hold values from 1.5 to 4
- cap: float32 [32768], P('dom'), may hold values from 0.05 to 0.5
- send_nodes: int32 [16, 16, 128], P('dom'), may hold values from 0 to 2047, as said below
- send_count: int32 [16, 16], P('dom'), may hold values from 0 to 128, as said below
- nl_nodes: int32 [16, 512], P('dom'), may hold values from 0 to 2047, as said below
- nl_count: int32 [16], P('dom'), may hold values from 1 to 512, 4096 in all
- op_wave: float32 [512, 8192], P(None, ('dom', 'harm')), may hold values from -1.5 to 1
- nl_gain: float32 [8192], P(('dom', 'harm')), may hold values from 0.1 to 1
Outputs:
- new_vector: float32 [2, 256, 32768], P(None, 'harm', 'dom')
- hess_column: float32 [21], replicated
Inputs may be any that keep to these rules, and one draw needn't show every extreme that they name: `send_count`: A partition s lists live nodes only for the partitions 1, 15, 8 and 9 places after it (modulo 16), never for itself, at least 32 for each of those, and exactly 128 for at least one of them. `send_nodes`: distinct local nodes within one list. `tile_cols`: every tile of the ghost part of each partition's extended vector is read by some row tile of that partition. `nl_nodes`: distinct local nodes within a partition. The basis vectors are linearly independent.
All inputs are finite; a program needn't handle non-finite values. No bound on the sum of `nl_count` on one device may be relied on, other than what follows from the above.
Results may differ from a plain program's by a relative error of at most 0.0003.
Values sent between devices are 32-bit elements; how exact they have to be, the bound alone decides.
No kernel may reach another device: no remote copies, remote signals or barrier semaphores. Data moves between devices by JAX's collectives and lax.ppermute only.
A program may use at most 128 MiB of HBM per device.

v0:
```python
import functools
import math

import jax
import jax.numpy as jnp
from jax import lax
from jax.sharding import Mesh
from jax.sharding import PartitionSpec as P

HARM = 256
DOM = ("dom_0", "dom_1")
HARM_AXES = ("harm_0", "harm_1")
DOM_HARM = ("dom_0", "dom_1", "harm_0", "harm_1")


epsilon = 1e-06


def cut_along(value, dim, length):
    before, after = (value.shape[:dim], value.shape[dim + 1 :])
    return jnp.moveaxis(value.reshape(*before, length, -1, *after), dim, 0)


def sent_and_summed(value, axis, dim):
    parts = cut_along(value, dim, lax.axis_size(axis))
    arrived = lax.all_to_all(parts, axis, split_axis=0, concat_axis=0, tiled=True)
    return arrived.sum(axis=0)


def copy_for_each(value, axis):
    length = lax.axis_size(axis)
    return lax.all_to_all(
        jnp.broadcast_to(value[None], (length, *value.shape)), axis, 0, 0, tiled=True
    )


def laid_out(parts, dim):
    parts = jnp.moveaxis(parts, 0, dim)
    dims = parts.shape
    return parts.reshape(*dims[:dim], dims[dim] * dims[dim + 1], *dims[dim + 2 :])


def gathered_copies(value, axis, dim):
    parts = copy_for_each(value, axis)
    return laid_out(parts, dim)


def over_axes(value, axes):
    return functools.reduce(lax.psum, axes, value)


def tables(harmonic, samples):
    sample_index = jnp.arange(samples, dtype=jnp.int32)
    product = harmonic[None, :] * sample_index[:, None] % samples
    angles = 2.0 * math.pi * product.astype(jnp.float32) / samples
    cosine = jnp.cos(angles)
    sine_part = jnp.sin(angles)
    alternating = 1.0 - 2.0 * (sample_index % 2).astype(jnp.float32)
    is_zero = harmonic == 0
    second = jnp.where(is_zero[None, :], alternating[:, None], sine_part)
    inverse = jnp.stack([cosine, second], axis=1)
    weights = jnp.where(is_zero, 1.0 / samples, 2.0 / samples).astype(jnp.float32)
    forward = jnp.transpose(
        jnp.stack([cosine * weights[None, :], second * weights[None, :]], axis=1), (1, 2, 0)
    )
    return (inverse, forward)


def solve_gram(gram_matrix, projections):
    factor = jnp.linalg.cholesky(gram_matrix)
    size_count = gram_matrix.shape[0]
    middle = jnp.zeros_like(projections)
    for index in range(size_count):
        middle = middle.at[index].set(
            (projections[index] - jnp.dot(factor[index], middle, precision=lax.Precision.HIGHEST))
            / factor[index, index]
        )
    answer = jnp.zeros_like(projections)
    for index in range(size_count - 1, -1, -1):
        answer = answer.at[index].set(
            (middle[index] - jnp.dot(factor[:, index], answer, precision=lax.Precision.HIGHEST))
            / factor[index, index]
        )
    return answer


def local(
    basis,
    coeffs,
    conductance_tiles,
    tile_cols,
    self_cond,
    cap,
    send_nodes,
    send_count,
    nl_nodes,
    nl_count,
    op_wave,
    nl_gain,
):
    highest_harmonic = lax.Precision.HIGHEST
    harm_local = basis.shape[2]
    node_dev = basis.shape[3]
    count_of_rows = 2 * harm_local
    peer_count = lax.axis_size(DOM)
    vector = jnp.einsum("b,bpkn->pkn", coeffs, basis, precision=highest_harmonic)
    flattened = vector.reshape(count_of_rows, node_dev)
    peer_cap = send_nodes.shape[2]
    active = jnp.arange(peer_cap, dtype=jnp.int32)[None, :] < send_count[0][:, None]
    packed = jnp.take(flattened, send_nodes[0].reshape(-1), axis=1).reshape(
        count_of_rows, peer_count, peer_cap
    )
    packed = jnp.where(active[None], packed, 0.0)
    ghosts = lax.all_to_all(packed, DOM, split_axis=1, concat_axis=1, tiled=True)
    tile_size = conductance_tiles.shape[2]
    local_tiles = node_dev // tile_size
    extended = jnp.concatenate(
        [flattened.reshape(count_of_rows, local_tiles, tile_size), ghosts], axis=1
    )
    picked_entries = jnp.take(extended, tile_cols, axis=1)
    coupled_nodes = jnp.einsum(
        "rhfq,hfqo->rho", picked_entries, conductance_tiles, precision=highest_harmonic
    ).reshape(2, harm_local, node_dev)
    harmonic = lax.axis_index(HARM_AXES) * harm_local + jnp.arange(harm_local, dtype=jnp.int32)
    angular = 2.0 * math.pi * harmonic.astype(jnp.float32) / HARM
    frequency = jnp.stack(
        [-angular[:, None] * cap[None, :] * vector[1], angular[:, None] * cap[None, :] * vector[0]]
    )
    base = coupled_nodes + self_cond[None, None, :] * vector + frequency
    nl_cap = nl_nodes.shape[1]
    nl_active = jnp.arange(nl_cap, dtype=jnp.int32) < nl_count[0]
    sampled = jnp.where(nl_active[None, None, :], jnp.take(vector, nl_nodes[0], axis=2), 0.0)
    samples = 2 * HARM
    node_conductance = nl_gain[None, :] * jnp.exp(op_wave)
    inverse, forward = tables(harmonic, samples)
    inverse_local = inverse.reshape(samples, count_of_rows)
    forward_local = forward.reshape(count_of_rows, samples)
    sampled_rows = sampled.reshape(count_of_rows, nl_cap)
    waveform_rows = sent_and_summed(
        jnp.einsum("cn,sc->ns", sampled_rows, inverse_local, precision=highest_harmonic),
        HARM_AXES,
        0,
    )
    current_rows = waveform_rows * node_conductance.T
    returned_rows = jnp.dot(
        gathered_copies(current_rows, HARM_AXES, 0), forward_local.T, precision=highest_harmonic
    )
    back_local = returned_rows.T.reshape(2, harm_local, nl_cap)
    back_local = jnp.where(nl_active[None, None, :], back_local, 0.0)
    product = base.at[:, :, nl_nodes[0]].add(back_local)
    gram_local = jnp.einsum("apkn,bpkn->ab", basis, basis, precision=highest_harmonic)
    proj_local = jnp.einsum("apkn,pkn->a", basis, product, precision=highest_harmonic)
    entries = count_of_rows * lax.axis_size(HARM_AXES) * node_dev * peer_count
    gram_matrix, projections, energy = (
        over_axes(gram_local, DOM_HARM),
        over_axes(proj_local, DOM_HARM),
        over_axes(jnp.sum(product * product), DOM_HARM),
    )
    hess = solve_gram(gram_matrix / entries, projections / entries)
    residual = product - jnp.einsum("a,apkn->pkn", hess, basis, precision=highest_harmonic)
    mean_square = (energy - jnp.dot(projections, hess, precision=highest_harmonic)) / entries
    norm_value = jnp.sqrt(mean_square + epsilon)
    return (residual / norm_value, jnp.concatenate([hess, norm_value[None]]))


def solution(mesh):
    split = Mesh(mesh.devices.reshape(4, 4, 4, 2), ("dom_0", "dom_1", "harm_0", "harm_1"))
    return jax.shard_map(
        local,
        mesh=split,
        in_specs=(
            P(None, None, HARM_AXES, DOM),
            P(),
            P(DOM, None, None, None),
            P(DOM, None),
            P(DOM),
            P(DOM),
            P(DOM, None, None),
            P(DOM, None),
            P(DOM, None),
            P(DOM),
            P(None, DOM_HARM),
            P(DOM_HARM),
        ),
        out_specs=(P(None, HARM_AXES, DOM), P()),
        check_vma=False,
    )
```

profile of v0, /device:TPU:1, one launch (start us, length us, event | category | flops | bytes accessed | tf_op | source)
XLA Modules:
  0.0 369.3 jit_solution(4464375951544975254)
XLA Ops:
  0.7 0.6 copy-done
  1.3 17.0 %fusion.2 = f32[1,2,32,2048]{3,0,2,1:T(1,128)S(1)} fusion(f32[20,2,32,2048]{3,2,1,0:T(8,128)} %param.92, f32[20]{0:T(128)S(1)} %copy-done), kind=kOutput, calls=%fused_computation.6 | convolution fusion | flops 31457280 | bytes 11010128 | tf_op jit(solution)/shard_map/b,bpkn->pkn/dot_general | solution.py:106
  18.5 0.6 copy-done.3
  19.5 5.5 %gather_fusion = f32[2048,64]{1,0:T(8,128)S(1)} fusion(f32[64,2048]{0,1:T(8,128)S(1)} %copy.94, s32[2048]{0:T(1024)S(1)} %broadcast_clamp_fusion), kind=kCustom, calls=%fused_computation | custom fusion | bytes 1056768 | tf_op jit(solution)/shard_map/jit(_take)/gather | solution.py:110
  25.4 0.9 select_select_fusion
  26.3 7.6 %all-to-all-start = ((f32[64,16,128]{2,0,1:T(8,128)}), f32[64,16,128]{2,0,1:T(8,128)S(1)}, u32[]{:S(2)}, u32[]{:S(2)}) async-start(f32[64,16,128]{2,0,1:T(8,128)} %select_select_fusion), calls=%async_computation | async-start | bytes 1048576 | tf_op jit(solution)/shard_map/all_to_all | solution.py:114
  34.0 2.3 copy.99
  36.3 3.1 gather_fusion.2
  40.7 1.0 broadcast_multiply_fusion
  41.7 2.0 fusion.90
  43.7 0.8 slice_multiply_fusion.1
  44.5 7.4 %all-to-all-start.1 = ((f32[8,64,512]{2,1,0:T(8,128)}), f32[8,64,512]{2,1,0:T(8,128)}, u32[]{:S(2)}, u32[]{:S(2)}) async-start(f32[8,64,512]{2,1,0:T(8,128)} %fusion.90), calls=%async_computation.1 | async-start | bytes 2097152 | tf_op jit(solution)/shard_map/all_to_all | solution.py:26
  52.4 0.7 copy.93
  53.1 29.8 %fusion.18 = f32[20,20]{0,1:T(8,128)S(1)} fusion(f32[20,2,32,2048]{3,2,1,0:T(8,128)} %param.92), kind=kOutput, calls=%fused_computation.23 | convolution fusion | flops 629145600 | bytes 10487360 | tf_op jit(solution)/shard_map/apkn,bpkn->ab/dot_general | solution.py:151
  83.0 2.4 gather_fusion.1
  85.4 1.5 reduce_sum.18
  86.9 1.0 bitcast_multiply_fusion
  87.9 1.1 broadcast_in_dim.132
  89.0 4.9 %all-to-all-start.2 = ((f32[8,64,512]{2,1,0:T(8,128)}), f32[8,64,512]{2,1,0:T(8,128)}, u32[]{:S(2)}, u32[]{:S(2)}) async-start(f32[8,64,512]{2,1,0:T(8,128)} %broadcast_in_dim.132), calls=%async_computation.2 | async-start | bytes 2097152 | tf_op jit(solution)/shard_map/all_to_all | solution.py:32
  93.9 6.6 %fusion.14 = f32[64,16,128]{2,0,1:T(8,128)S(1)} fusion(f32[16,6,128,128]{3,2,1,0:T(8,128)} %param.94, f32[16,6,64,128]{3,2,1,0:T(8,128)S(1)} %bitcast.304, pred[16,6]{1,0:T(8,128)(4,1)} %copy.93), kind=kOutput, calls=%fused_computation.20 | convolution fusion | flops 1208745984 | bytes 9961568 | tf_op jit(solution)/shard_map/rhfq,hfqo->rho/dot_general | solution.py:121
  100.9 1.4 maximum_add_fusion
  102.3 1.0 copy.102
  103.3 5.6 %all-to-all-done.2 = f32[8,64,512]{2,1,0:T(8,128)} async-done(((f32[8,64,512]{2,1,0:T(8,128)}), f32[8,64,512]{2,1,0:T(8,128)}, u32[]{:S(2)}, u32[]{:S(2)}) %all-to-all-start.2) | async-done | bytes 1048608 | tf_op jit(solution)/shard_map/all_to_all | solution.py:32
  108.9 2.3 fusion.17
  111.5 16.7 %scatter_fusion = f32[2,32,2048]{1,0,2:T(2,128)S(1)} fusion(f32[2,32,2048]{1,0,2:T(2,128)S(1)} %copy.102, s32[512]{0:T(512)S(1)} %bitcast.318, f32[512,2,32]{2,1,0:T(2,128)S(1)} %copy.103), kind=kCustom, calls=%fused_computation.3 | custom fusion | flops 32768 | bytes 395264 | tf_op jit(solution)/shard_map/scatter-add | solution.py:150
  128.2 2.8 multiply_reduce_fusion
  131.0 1.0 copy.113
  132.0 28.1 %fusion.21 = f32[20]{0:T(128)S(1)} fusion(f32[2,32,2048,1]{2,3,0,1:T(1,128)S(1)} %copy.113, f32[20,2,32,2048]{3,2,1,0:T(8,128)} %param.92), kind=kOutput, calls=%fused_computation.24 | convolution fusion | flops 31457280 | bytes 11010128 | tf_op jit(solution)/shard_map/apkn,pkn->a/dot_general | solution.py:152
  160.1 13.8 %all-reduce.4 = (f32[20]{0:T(128)S(1)}, f32[20,20]{0,1:T(8,128)S(1)}, f32[]{:T(128)}) all-reduce(f32[20]{0:T(128)S(1)} %fusion.21, f32[20,20]{0,1:T(8,128)S(1)} %fusion.18, f32[]{:T(128)} %multiply_reduce_fusion), channel_id=1, replica_groups=mesh['dom_0'=4,'dom_1'=4,'harm_0'=4,'harm_1'=2] {'dom_0'}, use_global_device_ids=true, to_apply=%region_2.3 | all-reduce | flops 421 | bytes 3368 | tf_op jit(solution)/shard_map/psum | solution.py:49
  173.9 14.2 %all-reduce.3 = (f32[20]{0:T(128)S(1)}, f32[20,20]{0,1:T(8,128)S(1)}, f32[]{:T(128)}) all-reduce(f32[20]{0:T(128)S(1)} %get-tuple-element.519, f32[20,20]{0,1:T(8,128)S(1)} %get-tuple-element.520, f32[]{:T(128)} %get-tuple-element.521), channel_id=1, replica_groups=mesh['dom_0'=4,'dom_1'=4,'harm_0'=4,'harm_1'=2] {'dom_1'}, use_global_device_ids=true, to_apply=%region_3.4 | all-reduce | flops 421 | bytes 3368 | tf_op jit(solution)/shard_map/psum | solution.py:49
  188.0 12.8 %all-reduce.2 = (f32[20]{0:T(128)S(1)}, f32[20,20]{0,1:T(8,128)S(1)}, f32[]{:T(128)}) all-reduce(f32[20]{0:T(128)S(1)} %get-tuple-element.516, f32[20,20]{0,1:T(8,128)S(1)} %get-tuple-element.517, f32[]{:T(128)} %get-tuple-element.518), channel_id=1, replica_groups=mesh['dom_0'=4,'dom_1'=4,'harm_0'=4,'harm_1'=2] {'harm_0'}, use_global_device_ids=true, to_apply=%region_4.5 | all-reduce | flops 421 | bytes 3368 | tf_op jit(solution)/shard_map/psum | solution.py:49
  200.8 16.4 %all-reduce.5 = (f32[20]{0:T(128)S(1)}, f32[20,20]{0,1:T(8,128)S(1)}, f32[]{:T(128)}) all-reduce(f32[20]{0:T(128)S(1)} %get-tuple-element.513, f32[20,20]{0,1:T(8,128)S(1)} %get-tuple-element.514, f32[]{:T(128)} %get-tuple-element.515), channel_id=1, replica_groups=mesh['dom_0'=4,'dom_1'=4,'harm_0'=4,'harm_1'=2] {'harm_1'}, use_global_device_ids=true, to_apply=%region_5.6 | all-reduce | flops 421 | bytes 3368 | tf_op jit(solution)/shard_map/psum | solution.py:49
  217.8 0.7 fusion.89
  218.6 1.8 cholesky.18
  220.5 0.6 compare_reduce_fusion
  221.1 0.6 select_select_fusion.1
  221.8 0.7 fusion.78
  225.7 0.7 fusion.87
  229.0 1.4 fusion.74
  232.4 1.4 fusion.72
  235.7 1.3 fusion.70
  238.8 1.3 fusion.68
  242.0 1.4 fusion.66
  245.3 1.3 fusion.64
  248.5 1.4 fusion.62
  251.9 1.3 fusion.60
  255.1 1.3 fusion.58
  258.5 1.4 fusion.56
  261.9 1.4 fusion.54
  265.2 1.3 fusion.52
  268.4 1.4 fusion.50
  271.8 1.3 fusion.48
  275.0 1.4 fusion.46
  278.3 1.3 fusion.44
  281.5 1.3 fusion.42
  284.7 1.3 fusion.80
  286.0 0.7 fusion.88
  290.7 0.7 multiply_reduce_fusion.20
  292.7 0.6 multiply_reduce_fusion.19
  297.8 0.6 multiply_reduce_fusion.17
  338.8 17.2 %fusion = f32[1,2,32,2048]{3,0,2,1:T(1,128)S(1)} fusion(f32[20,2,32,2048]{3,2,1,0:T(8,128)} %param.92, f32[20]{0:T(128)S(1)} %constant_dynamic-update-slice_fusion.36), kind=kOutput, calls=%fused_computation.4 | convolution fusion | flops 31457280 | bytes 11010128 | tf_op jit(solution)/shard_map/a,apkn->pkn/dot_general | solution.py:160
  356.6 2.3 copy.197
  360.3 4.4 %fusion.11 = f32[2,32,2048]{1,0,2:T(2,128)} fusion(f32[2,32,2048]{1,0,2:T(2,128)S(1)} %scatter_fusion, f32[1,2,32,2048]{2,1,3,0:T(2,128)} %copy.197, f32[]{:T(128)} %sqrt.3), kind=kLoop, calls=%fused_computation.16 | loop fusion | flops 262144 | bytes 1572868 | tf_op jit(solution)/shard_map/div | solution.py:163
  364.7 3.8 %copy.108 = f32[2,32,2048]{2,1,0:T(8,128)} copy(f32[2,32,2048]{1,0,2:T(2,128)} %fusion.11) | data formatting | bytes 1048576
  (129 shorter events, 17.6 us)
Async XLA Ops:
  0.6 0.7 copy-start
  0.6 18.8 %copy-start.6 = (s32[1,16,128]{2,1,0:T(8,128)S(1)}, s32[1,16,128]{2,1,0:T(8,128)}, u32[]{:S(2)}) copy-start(s32[1,16,128]{2,1,0:T(8,128)} %param.98) | copy-start | bytes 24580
  18.3 0.8 copy-start.3
  19.5 5.8 %copy-start.15 = (s32[1,16]{1,0:T(1,128)S(1)}, s32[1,16]{1,0:T(1,128)}, u32[]{:S(2)}) copy-start(s32[1,16]{1,0:T(1,128)} %param.99) | copy-start | bytes 196
  19.5 14.4 %copy-start.9 = (s32[16,6]{0,1:T(8,128)S(1)}, s32[16,6]{0,1:T(8,128)}, u32[]{:S(2)}) copy-start(s32[16,6]{0,1:T(8,128)} %param.95) | copy-start | bytes 1156
  19.5 14.4 %copy-start.12 = (s32[1,512]{1,0:T(1,128)S(1)}, s32[1,512]{1,0:T(1,128)}, u32[]{:S(2)}) copy-start(s32[1,512]{1,0:T(1,128)} %param.100) | copy-start | bytes 6148
  26.3 18.2 %all-to-all-start = ((f32[64,16,128]{2,0,1:T(8,128)}), f32[64,16,128]{2,0,1:T(8,128)S(1)}, u32[]{:S(2)}, u32[]{:S(2)}) async-start(f32[64,16,128]{2,0,1:T(8,128)} %select_select_fusion), calls=%async_computation | async-start | bytes 1048576 | tf_op jit(solution)/shard_map/all_to_all | solution.py:114
  33.9 9.8 %copy-start.10 = (f32[2048]{0:T(1024)S(1)}, f32[2048]{0:T(1024)}, u32[]{:S(2)}) copy-start(f32[2048]{0:T(1024)} %param.97) | copy-start | bytes 24580
  34.0 2.3 copy-start.7
  40.2 0.5 copy-start.13
  44.5 40.9 %all-to-all-start.1 = ((f32[8,64,512]{2,1,0:T(8,128)}), f32[8,64,512]{2,1,0:T(8,128)}, u32[]{:S(2)}, u32[]{:S(2)}) async-start(f32[8,64,512]{2,1,0:T(8,128)} %fusion.90), calls=%async_computation.1 | async-start | bytes 2097152 | tf_op jit(solution)/shard_map/all_to_all | solution.py:26
  85.4 8.4 %copy-start.1 = (f32[96,64,128]{2,1,0:T(8,128)S(1)}, f32[96,64,128]{2,1,0:T(8,128)}, u32[]{:S(2)}) copy-start(f32[96,64,128]{2,1,0:T(8,128)} %gather_fusion.1) | copy-start | bytes 9437188
  89.0 19.9 %all-to-all-start.2 = ((f32[8,64,512]{2,1,0:T(8,128)}), f32[8,64,512]{2,1,0:T(8,128)}, u32[]{:S(2)}, u32[]{:S(2)}) async-start(f32[8,64,512]{2,1,0:T(8,128)} %broadcast_in_dim.132), calls=%async_computation.2 | async-start | bytes 2097152 | tf_op jit(solution)/shard_map/all_to_all | solution.py:32
  93.9 7.0 %copy-start.11 = (f32[2048]{0:T(1024)S(1)}, f32[2048]{0:T(1024)}, u32[]{:S(2)}) copy-start(f32[2048]{0:T(1024)} %param.96) | copy-start | bytes 24580
  100.8 8.2 %copy-start.4 = (f32[512,1,32]{0,2,1:T(8,128)S(1)}, f32[512,1,32]{0,2,1:T(8,128)}, u32[]{:S(2)}) copy-start(f32[512,1,32]{0,2,1:T(8,128)} %get-tuple-element.548) | copy-start | bytes 196612
  100.8 8.2 %copy-start.5 = (f32[512,1,32]{0,2,1:T(8,128)S(1)}, f32[512,1,32]{0,2,1:T(8,128)}, u32[]{:S(2)}) copy-start(f32[512,1,32]{0,2,1:T(8,128)} %get-tuple-element.550) | copy-start | bytes 196612
  100.8 8.2 %copy-start.14 = (pred[512]{0:T(512)(128)(4,1)S(1)}, pred[512]{0:T(512)(128)(4,1)}, u32[]{:S(2)}) copy-start(pred[512]{0:T(512)(128)(4,1)} %copy-done.13) | copy-start | bytes 1540
  100.9 10.6 %copy-start.8 = (s32[512,1]{0,1:T(1,128)S(1)}, s32[512,1]{0,1:T(1,128)}, u32[]{:S(2)}) copy-start(s32[512,1]{0,1:T(1,128)} %copy-done.7) | copy-start | bytes 6148
  221.8 7.2 %copy-start.2 = (f32[20,20]{1,0:T(8,128)}, f32[20,20]{1,0:T(8,128)S(1)}, u32[]{:S(2)}) copy-start(f32[20,20]{1,0:T(8,128)S(1)} %select_select_fusion.1) | copy-start | bytes 4804
where the time goes:
time: 376 us; the launch traced here: 369 us
  matrix products  103 us (27%)
  between operations  79.5 us (21%)
  other arithmetic  72.4 us (19%)
  blocking collectives  57.1 us (15%)
  local copies, waits for them, and re-layouts  31.8 us (8%)
  starting transfers between devices  19.9 us (5%)
  waiting for transfers between devices  5.6 us (1%)
    psum x4, blocking collectives, over_axes(): return functools.reduce(lax.psum, axes, value)  57.1 us
    dot_general x1, matrix products, local(): jnp.einsum('apkn,bpkn->ab', basis, basis, precision=highest_harmonic)  29.8 us
    dot_general x1, matrix products, local(): jnp.einsum('apkn,pkn->a', basis, product, precision=highest_harmonic)  28.1 us
    dot_general x20, other arithmetic, solve_gram(): jnp.dot(factor[index], middle, precision=lax.Precision.HIGHEST)  25.3 us
    dot_general x1, matrix products, local(): jnp.einsum('a,apkn->pkn', hess, basis, precision=highest_harmonic)  17.2 us
    dot_general x1, matrix products, local(): jnp.einsum('b,bpkn->pkn', coeffs, basis, precision=highest_harmonic)  17 us
    scatter-add x1, other arithmetic, local(): product = base.at[:, :, nl_nodes[0]].add(back_local)  16.7 us
    dot_general x20, other arithmetic, solve_gram(): jnp.dot(factor[:, index], answer, precision=lax.Precision.HIGHEST)  12.1 us
  transfers between devices with their start and end apart: 3, of which 1 were waited for; matrix products, arithmetic and copies ran while one was open for 14% of the time, Pallas kernels for 0%

commit v1 on v0

v1 whole, which is shorter than its diff:
```python
import functools
import math

import ml_dtypes
import numpy as np

import jax
import jax.numpy as jnp
from jax import lax
from jax.experimental import pallas as pl
from jax.experimental.pallas import tpu as pltpu
from jax.sharding import Mesh
from jax.sharding import PartitionSpec as P

HARM = 256
SAMPLES = 2 * HARM
DOM = ("dom_0", "dom_1")
HARM_AXES = ("harm_0", "harm_1")
DOM_HARM = ("dom_0", "dom_1", "harm_0", "harm_1")
PEERS = (1, 15, 8, 9)
EPSILON = 1e-06

F32 = jnp.float32
BF16 = jnp.bfloat16


def halves(value):
    high = value.astype(BF16)
    return high, (value - high.astype(F32)).astype(BF16)


def thirds(value):
    high = value.astype(BF16)
    rest = value - high.astype(F32)
    middle = rest.astype(BF16)
    return high, middle, (rest - middle.astype(F32)).astype(BF16)


def mm(left, right):
    return jnp.dot(left, right, preferred_element_type=F32)


def mm_nt(left, right):
    return lax.dot_general(left, right, (((1,), (1,)), ((), ())), preferred_element_type=F32)


def split_table(table):
    high = table.astype(ml_dtypes.bfloat16)
    low = (table - high.astype(np.float64)).astype(ml_dtypes.bfloat16)
    return [high, low]


def transform_tables():
    index = np.arange(HARM)
    angle = 2.0 * np.pi * ((index[:, None] * index[None, :]) % SAMPLES) / SAMPLES
    cosine, sine = np.cos(angle), np.sin(angle)
    sine[:, 0] = 1.0 - 2.0 * (index % 2)
    return np.stack(split_table(cosine) + split_table(sine) + split_table(sine.T))


def pair_list(count):
    return [(i, j) for i in range(count) for j in range(i, count)]


def unpack_tables(count, rows, width):
    pairs = pair_list(count)
    mask = np.zeros((2, rows, width), np.float32)
    place = np.zeros((2, width, 128), np.float32)
    for position, (i, j) in enumerate(pairs):
        mask[0, i, position] = 1.0
        place[0, position, j] = 1.0
        if i != j:
            mask[1, j, position] = 1.0
            place[1, position, i] = 1.0
    for i in range(count):
        mask[0, i, len(pairs) + i] = 1.0
        place[0, len(pairs) + i, count] = 1.0
    return mask, place.astype(ml_dtypes.bfloat16)


def basis_copy(source, target, sems, block):
    rows = pl.ds(pl.multiple_of(block * 8, 8), 8)
    return pltpu.make_async_copy(source.at[:, rows, :], target.at[:, rows, :], sems.at[block])


def start_all(source, target, sems):
    for block in range(target.shape[1] // 8):
        basis_copy(source, target, sems, block).start()


def row_total(rows_ref):
    ones = jnp.ones((8, rows_ref.shape[1]), BF16)
    return sum(mm_nt(ones, part) for part in thirds(rows_ref[...]))


def vector_kernel(coeffs, send_count, nl_count, send_nodes, nl_nodes, basis_hbm,
                  vector, ghost_0, ghost_1, ghost_2, ghost_3, sampled,
                  basis, select, sems):
    start_all(basis_hbm, basis, sems)
    count, rows, nodes = basis.shape
    peers = send_nodes.shape[0]
    slots = nl_nodes.shape[1]
    cap = send_nodes.shape[1]
    me = lax.axis_index(DOM)
    lane = lax.broadcasted_iota(jnp.int32, (1, cap), 1)
    wanted = []
    for step in PEERS:
        peer = lax.rem(me + step, peers)
        listed = send_nodes[pl.ds(peer, 1), :]
        wanted.append(jnp.where(lane < send_count[peer], listed, -1))
    slot = lax.broadcasted_iota(jnp.int32, (1, slots), 1)
    wanted.append(jnp.where(slot < nl_count[0], nl_nodes[...], -1))
    columns = jnp.concatenate(wanted, axis=1)
    chunk = nodes // (rows // 8)

    @pl.loop(0, rows // 8)
    def _(block):
        start = pl.multiple_of(block * chunk, chunk)
        node = lax.broadcasted_iota(jnp.int32, (chunk, columns.shape[1]), 0) + start
        select[pl.ds(start, chunk), :] = jnp.where(node == columns, 1.0, 0.0).astype(BF16)
        basis_copy(basis_hbm, basis, sems, block).wait()
        part = pl.ds(pl.multiple_of(block * 8, 8), 8)
        total = coeffs[0] * basis[0, part, :]
        for j in range(1, count):
            total = total + coeffs[j] * basis[j, part, :]
        vector[part, :] = total

    left = jnp.concatenate(halves(vector[...]), axis=0)
    for peer, ghost in enumerate((ghost_0, ghost_1, ghost_2, ghost_3)):
        taken = mm(left, select[:, peer * cap : (peer + 1) * cap])
        ghost[...] = taken[:rows] + taken[rows:]
    half = rows // 2
    low_lanes = lax.broadcasted_iota(jnp.int32, (half, 128), 1) < 64
    for pair in range(slots // 128):
        first = len(PEERS) * cap + pair * 128
        taken = mm(left, select[:, first : first + 128])
        taken = taken[:rows] + taken[rows:]
        top, bottom = taken[:half], taken[half:]
        sampled[2 * pair] = jnp.where(low_lanes, top, pltpu.roll(bottom, 64, 1))
        sampled[2 * pair + 1] = jnp.where(low_lanes, pltpu.roll(top, 64, 1), bottom)


def gram_kernel(basis_hbm, packed, basis, sums, totals, sems):
    start_all(basis_hbm, basis, sems)
    count, rows, nodes = basis.shape
    position = {pair: p for p, pair in enumerate(pair_list(count))}
    group = 5
    groups = [range(g, g + group) for g in range(0, count, group)]
    sums[...] = jnp.zeros_like(sums)

    @pl.loop(0, rows // 8)
    def _(block):
        basis_copy(basis_hbm, basis, sems, block).wait()
        part = pl.ds(pl.multiple_of(block * 8, 8), 8)
        for x, left in enumerate(groups):
            for right in groups[x:]:
                names = [(i, j) for i in left for j in right if i <= j]
                held = {}
                for chunk in range(nodes // 128):
                    lanes = slice(chunk * 128, (chunk + 1) * 128)
                    value = {i: basis[i, part, lanes] for i in set(left) | set(right)}
                    for i, j in names:
                        term = value[i] * value[j]
                        held[i, j] = held[i, j] + term if chunk else term
                for pair in names:
                    sums[position[pair]] += held[pair]

    totals[...] = jnp.zeros_like(totals)
    for p in range(len(position)):
        totals[p : p + 1, :] = jnp.sum(sums[p], axis=0, keepdims=True)
    packed[...] = row_total(totals)


def current_kernel(arrived, wave, gain, tables, leaving):
    half = HARM // 2
    spectrum = arrived[...].reshape(HARM, 128)
    lane = lax.broadcasted_iota(jnp.int32, (HARM, 128), 1)
    harmonic = lax.broadcasted_iota(jnp.int32, (HARM, 128), 0)
    low = lane < 64
    sign = jnp.where(harmonic % 2 == 0, 1.0, -1.0)
    swapped = pltpu.roll(spectrum, 64, 1)
    even = jnp.where(low, spectrum, swapped * sign)
    odd = jnp.where(low, swapped, spectrum * sign)

    def product(index, values):
        high, lower = values
        return (
            mm(tables[index], high) + mm(tables[index], lower) + mm(tables[index + 1], high)
        )

    waveform = product(0, halves(even)) + product(2, halves(odd))
    gains = jnp.concatenate([gain[...], gain[...]], axis=1)
    growth = jnp.exp(jnp.concatenate([wave[:HARM], wave[HARM:]], axis=1))
    current = halves(gains * growth * waveform)
    weight = jnp.where(harmonic == 0, 1.0 / SAMPLES, 2.0 / SAMPLES)
    cosine = product(0, current)
    sine = product(4, current)
    result = weight * jnp.where(
        low,
        cosine + sign * pltpu.roll(cosine, 64, 1),
        sign * sine + pltpu.roll(sine, 64, 1),
    )
    leaving[...] = result.reshape(leaving.shape)


def coupling_kernel(tile_cols, vector, ghost_0, ghost_1, ghost_2, ghost_3,
                    self_cond, cap, tiles, base, extended):
    rows, nodes = vector.shape
    half = rows // 2
    local_tiles = nodes // 128
    peers = extended.shape[0] - local_tiles
    step = pl.program_id(0)
    me = lax.axis_index(DOM)

    @pl.when(step == 0)
    def _():
        for tile in range(local_tiles):
            high, low = halves(vector[:, tile * 128 : (tile + 1) * 128])
            extended[tile, :rows] = high
            extended[tile, rows:] = low
        extended[local_tiles:] = jnp.zeros((peers, 2 * rows, 128), BF16)
        for jump, ghost in zip(PEERS, (ghost_0, ghost_1, ghost_2, ghost_3)):
            sender = local_tiles + lax.rem(me + peers - jump, peers)
            high, low = halves(ghost[...])
            extended[sender, :rows] = high
            extended[sender, rows:] = low

    per_step, terms = tiles.shape[0], tiles.shape[1]
    first = lax.axis_index(HARM_AXES) * half
    harmonic = first + lax.broadcasted_iota(jnp.int32, (half, 128), 0)
    angular = (2.0 * math.pi / HARM) * harmonic.astype(F32)
    for t in range(per_step):
        row = step * per_step + t
        total = jnp.zeros((rows, 128), F32)
        for i in range(0, terms, 2):
            left = jnp.concatenate(
                [extended[tile_cols[row, i]], extended[tile_cols[row, i + 1]]], axis=1
            )
            high, low = halves(tiles[t, i : i + 2].reshape(256, 128))
            main = mm(left, high)
            total = total + main[:rows] + main[rows:] + mm(left[:rows], low)
        lanes = pl.ds(pl.multiple_of(row * 128, 128), 128)
        cosine, sine = vector[:half, lanes], vector[half:, lanes]
        ground, reactive = self_cond[:, lanes], angular * cap[:, lanes]
        base[:half, lanes] = total[:half] + ground * cosine - reactive * sine
        base[half:, lanes] = total[half:] + ground * sine + reactive * cosine


def product_kernel(nl_count, nl_nodes, arrived, base, packed_gram, basis_hbm,
                   product, packed, basis, totals, sems):
    start_all(basis_hbm, basis, sems)
    count, rows, nodes = basis.shape
    half = rows // 2
    slots = nl_nodes.shape[1]
    slot = lax.broadcasted_iota(jnp.int32, (1, slots), 1)
    columns = jnp.where(slot < nl_count[0], nl_nodes[...], -1)
    low_lanes = lax.broadcasted_iota(jnp.int32, (half, 128), 1) < 64
    top, bottom = [], []
    for pair in range(slots // 128):
        even, odd = arrived[2 * pair], arrived[2 * pair + 1]
        top.append(jnp.where(low_lanes, even, pltpu.roll(odd, 64, 1)))
        bottom.append(jnp.where(low_lanes, pltpu.roll(even, 64, 1), odd))
    returned = jnp.concatenate(
        [jnp.concatenate(top, axis=1), jnp.concatenate(bottom, axis=1)], axis=0
    )
    left = jnp.concatenate(halves(returned), axis=0)
    width = 256
    for start in range(0, nodes, width):
        node = lax.broadcasted_iota(jnp.int32, (width, slots), 0) + start
        chosen = jnp.where(node == columns, 1.0, 0.0).astype(BF16)
        added = mm_nt(left, chosen)
        lanes = slice(start, start + width)
        product[:, lanes] = base[:, lanes] + added[:rows] + added[rows:]

    def block_sums(block, sums):
        basis_copy(basis_hbm, basis, sems, block).wait()
        part = pl.ds(pl.multiple_of(block * 8, 8), 8)
        sums = list(sums)
        for chunk in range(nodes // 128):
            lanes = slice(chunk * 128, (chunk + 1) * 128)
            value = product[part, lanes]
            for a in range(count):
                sums[a] = sums[a] + basis[a, part, lanes] * value
            sums[count] = sums[count] + value * value
        return tuple(sums)

    sums = lax.fori_loop(
        0, rows // 8, block_sums, tuple(jnp.zeros((8, 128), F32) for _ in range(count + 1))
    )
    totals[...] = jnp.zeros_like(totals)
    first = count * (count + 1) // 2
    for a in range(count + 1):
        totals[first + a : first + a + 1, :] = jnp.sum(sums[a], axis=0, keepdims=True)
    line = (row_total(totals) + packed_gram[...])[:1]
    both = jnp.concatenate([line[:, :128], line[:, 128:]], axis=0)
    packed[...] = jnp.broadcast_to(both[None], packed.shape)


def residual_kernel(entries, gathered, mask, place, product, basis_hbm,
                    residual, column, basis, weights, sems):
    start_all(basis_hbm, basis, sems)
    count, rows, nodes = basis.shape
    height = mask.shape[1]
    scale = 1.0 / entries
    summed = jnp.sum(gathered[...], axis=0) * scale
    line = jnp.concatenate([summed[:1], summed[1:]], axis=1)
    system = jnp.zeros((height, 128), F32)
    for side in range(2):
        spread = mask[side] * line
        for part in thirds(spread):
            system = system + mm(part, place[side])
    lane = lax.broadcasted_iota(jnp.int32, (height, 128), 1)
    row = lax.broadcasted_iota(jnp.int32, (height, 128), 0)
    proj = jnp.sum(jnp.where(lane == count, system, 0.0), axis=1, keepdims=True)
    work = system
    for k in range(count):
        pivot_row = work[k : k + 1, :]
        pivot = pivot_row[:, k : k + 1]
        scaled = pivot_row / pivot
        work = jnp.where(row == k, scaled, work - work[:, k : k + 1] * scaled)
    solved = work[:, count : count + 1]
    solved = jnp.where(row[:, :1] < count, solved, 0.0)
    first = count * (count + 1) // 2
    energy = line[:, first + count : first + count + 1]
    mean_square = energy - jnp.sum(proj * solved, axis=0, keepdims=True)
    norm = jnp.sqrt(mean_square + EPSILON)
    wide = jnp.broadcast_to(solved, (height, 128))
    as_row = jnp.sum(jnp.where(lane == row, wide, 0.0), axis=0, keepdims=True)
    as_row = jnp.where(lane[:1] == count, norm, as_row)
    column[...] = as_row[:, : count + 1]
    weights[...] = wide
    inverse = jnp.broadcast_to(1.0 / norm, (8, 128))

    @pl.loop(0, rows // 8)
    def _(block):
        basis_copy(basis_hbm, basis, sems, block).wait()
        part = pl.ds(pl.multiple_of(block * 8, 8), 8)
        hess = [jnp.broadcast_to(weights[a : a + 1, :], (8, 128)) for a in range(count)]
        for chunk in range(nodes // 128):
            lanes = slice(chunk * 128, (chunk + 1) * 128)
            terms = [hess[a] * basis[a, part, lanes] for a in range(count)]
            while len(terms) > 1:
                terms = [sum(terms[i : i + 2]) for i in range(0, len(terms), 2)]
            residual[part, lanes] = (product[part, lanes] - terms[0]) * inverse


def local(
    basis,
    coeffs,
    conductance_tiles,
    tile_cols,
    self_cond,
    cap,
    send_nodes,
    send_count,
    nl_nodes,
    nl_count,
    op_wave,
    nl_gain,
):
    count, _, harm_local, nodes = basis.shape
    rows = 2 * harm_local
    peers = lax.axis_size(DOM)
    groups = lax.axis_size(HARM_AXES)
    peer_cap = send_nodes.shape[2]
    nl_cap = nl_nodes.shape[1]
    basis = basis.reshape(count, rows, nodes)
    smem = pl.BlockSpec(memory_space=pltpu.SMEM)
    vmem = pl.BlockSpec(memory_space=pltpu.VMEM)
    hbm = pl.BlockSpec(memory_space=pl.ANY)
    shape = jax.ShapeDtypeStruct
    basis_scratch = pltpu.VMEM((count, rows, nodes), F32)
    sems = pltpu.SemaphoreType.DMA((rows // 8,))
    basis_bytes = 4 * count * rows * nodes

    def cost(flops, size):
        return pl.CostEstimate(flops=flops, bytes_accessed=size, transcendentals=0)

    vector, *ghosts, sampled = pl.pallas_call(
        vector_kernel,
        out_shape=[shape((rows, nodes), F32)]
        + [shape((rows, peer_cap), F32)] * len(PEERS)
        + [shape((groups, harm_local, 128), F32)],
        in_specs=[smem, smem, smem, vmem, vmem, hbm],
        out_specs=[vmem] * (2 + len(PEERS)),
        scratch_shapes=[
            basis_scratch,
            pltpu.VMEM((nodes, len(PEERS) * peer_cap + nl_cap), BF16),
            sems,
        ],
        cost_estimate=cost(10**9, basis_bytes),
        name="vector",
    )(coeffs, send_count[0], nl_count, send_nodes[0], nl_nodes, basis)

    arrived_spectrum = lax.all_to_all(sampled, HARM_AXES, 0, 0, tiled=True)
    ghosts = [
        lax.ppermute(ghost, DOM, [(i, (i + jump) % peers) for i in range(peers)])
        for jump, ghost in zip(PEERS, ghosts)
    ]

    width = 256
    packed_gram = pl.pallas_call(
        gram_kernel,
        out_shape=shape((8, width), F32),
        in_specs=[hbm],
        out_specs=vmem,
        scratch_shapes=[
            basis_scratch,
            pltpu.VMEM((count * (count + 1) // 2, 8, 128), F32),
            pltpu.VMEM((width, 128), F32),
            sems,
        ],
        cost_estimate=cost(10**9, basis_bytes),
        name="gram",
    )(basis)

    leaving = pl.pallas_call(
        current_kernel,
        out_shape=shape((groups, harm_local, 128), F32),
        in_specs=[vmem] * 4,
        out_specs=vmem,
        cost_estimate=cost(4 * 10**8, 2 * 10**6),
        name="current",
    )(arrived_spectrum, op_wave, nl_gain.reshape(1, -1), jnp.asarray(transform_tables()))

    returned = lax.all_to_all(leaving, HARM_AXES, 0, 0, tiled=True)

    tile_rows, terms = tile_cols.shape
    per_step = 2
    whole = lambda *dims: pl.BlockSpec(dims, lambda i: (0,) * len(dims))
    base = pl.pallas_call(
        coupling_kernel,
        grid=(tile_rows // per_step,),
        out_shape=shape((rows, nodes), F32),
        in_specs=[smem, whole(rows, nodes)]
        + [whole(rows, peer_cap)] * len(PEERS)
        + [
            whole(1, nodes),
            whole(1, nodes),
            pl.BlockSpec((per_step, terms, 128, 128), lambda i: (i, 0, 0, 0)),
        ],
        out_specs=whole(rows, nodes),
        scratch_shapes=[pltpu.VMEM((nodes // 128 + peers, 2 * rows, 128), BF16)],
        cost_estimate=cost(10**9, 4 * tile_rows * terms * 128 * 128),
        name="coupling",
    )(
        tile_cols, vector, *ghosts, self_cond.reshape(1, -1), cap.reshape(1, -1),
        conductance_tiles,
    )

    devices = peers * groups
    product, packed = pl.pallas_call(
        product_kernel,
        out_shape=[shape((rows, nodes), F32), shape((devices, width // 128, 128), F32)],
        in_specs=[smem, vmem, vmem, vmem, vmem, hbm],
        out_specs=[vmem, vmem],
        scratch_shapes=[
            basis_scratch,
            pltpu.VMEM((width, 128), F32),
            sems,
        ],
        cost_estimate=cost(10**9, basis_bytes),
        name="product",
    )(nl_count, nl_nodes, returned, base, packed_gram, basis)

    gathered = lax.all_to_all(packed, DOM_HARM, 0, 0, tiled=True)

    entries = rows * groups * nodes * peers
    mask, place = unpack_tables(count, 24, width)
    residual, column = pl.pallas_call(
        functools.partial(residual_kernel, float(entries)),
        out_shape=[shape((rows, nodes), F32), shape((1, count + 1), F32)],
        in_specs=[vmem, vmem, vmem, vmem, hbm],
        out_specs=[vmem, vmem],
        scratch_shapes=[basis_scratch, pltpu.VMEM((24, 128), F32), sems],
        cost_estimate=cost(10**9, basis_bytes),
        name="residual",
    )(gathered, jnp.asarray(mask), jnp.asarray(place), product, basis)
    return (residual.reshape(2, harm_local, nodes), column.reshape(count + 1))


def solution(mesh):
    split = Mesh(mesh.devices.reshape(4, 4, 4, 2), ("dom_0", "dom_1", "harm_0", "harm_1"))
    return jax.shard_map(
        local,
        mesh=split,
        in_specs=(
            P(None, None, HARM_AXES, DOM),
            P(),
            P(DOM, None, None, None),
            P(DOM, None),
            P(DOM),
            P(DOM),
            P(DOM, None, None),
            P(DOM, None),
            P(DOM, None),
            P(DOM),
            P(None, DOM_HARM),
            P(DOM_HARM),
        ),
        out_specs=(P(None, HARM_AXES, DOM), P()),
        check_vma=False,
    )
```

time: 376 us -> 83 us (0.22); the launches traced: 369 us -> 82.5 us
  matrix products: 103 us -> 0 us
  between operations: 79.5 us -> 1.42 us
  other arithmetic: 72.4 us -> 0 us
  Pallas kernels: 0 us -> 40 us
  blocking collectives: 57.1 us -> 18.8 us
  local copies, waits for them, and re-layouts: 31.8 us -> 3.44 us
  waiting for transfers between devices: 5.6 us -> 0.02 us
    dot_general x7 -> x0, matrix products: 103 us -> none  [the longest x1 29.8 us: local(): jnp.einsum('apkn,bpkn->ab', basis, basis, precision=highest_harmonic)]
    psum x4 -> x0, blocking collectives: 57.1 us -> none  [over_axes(): return functools.reduce(lax.psum, axes, value)]
    pallas_call x0 -> x6, Pallas kernels: none -> 40 us  [the longest x1 9.67 us: local(): pl.pallas_call(gram_kernel, out_shape=shape((8, width), F32), in_specs=[h...]
    dot_general x41 -> x0, other arithmetic: 38 us -> none  [the longest x20 25.3 us: solve_gram(): jnp.dot(factor[index], middle, precision=lax.Precision.HIGHEST)]
    all_to_all x0 -> x1, blocking collectives: none -> 18.8 us  [local(): gathered = lax.all_to_all(packed, DOM_HARM, 0, 0, tiled=True)]
    scatter-add x1 -> x0, other arithmetic: 16.7 us -> none  [local(): product = base.at[:, :, nl_nodes[0]].add(back_local)]
    gather x5 -> x0, local copies, waits for them, and re-layouts: 11.5 us -> none  [the longest x2 5.78 us: local(): jnp.take(flattened, send_nodes[0].reshape(-1), axis=1)]
    all_to_all x3 -> x2, starting transfers between devices: 19.9 us -> 12.5 us  [the longest x1 6.82 us: local(): arrived_spectrum = lax.all_to_all(sampled, HARM_AXES, 0, 0, tiled=True)]
  transfers between devices with their start and end apart: 3 -> 6, of which waited for: 1 -> 0; matrix products, arithmetic and copies ran while one was open for 14% -> 2% of each run, Pallas kernels for 0% -> 24%
where the time goes in v1:
time: 83 us; the launch traced here: 82.5 us
  Pallas kernels  40 us (48%)
  starting transfers between devices  18.8 us (23%)
  blocking collectives  18.8 us (23%)
  local copies, waits for them, and re-layouts  3.44 us (4%)
  between operations  1.42 us (2%)
    all_to_all x1, blocking collectives, local(): gathered = lax.all_to_all(packed, DOM_HARM, 0, 0, tiled=True)  18.8 us
    pallas_call x1, Pallas kernels, local(): pl.pallas_call(gram_kernel, out_shape=shape((8, width), F32), in_specs=[h...  9.67 us
    pallas_call x1, Pallas kernels, local(): pl.pallas_call(coupling_kernel, grid=(tile_rows // per_step,), out_shape=...  7.58 us
    pallas_call x1, Pallas kernels, local(): pl.pallas_call(vector_kernel, out_shape=[shape((rows, nodes), F32)] + [sh...  7.04 us
    all_to_all x1, starting transfers between devices, local(): arrived_spectrum = lax.all_to_all(sampled, HARM_AXES, 0, 0, tiled=True)  6.82 us
    pallas_call x1, Pallas kernels, local(): pl.pallas_call(functools.partial(residual_kernel, float(entries)), out_sh...  6.73 us
    ppermute x4, starting transfers between devices, local(): lax.ppermute(ghost, DOM, [(i, (i + jump) % peers) for i in range(peers)])  6.32 us
    pallas_call x1, Pallas kernels, local(): pl.pallas_call(product_kernel, out_shape=[shape((rows, nodes), F32), shap...  6.23 us
  transfers between devices with their start and end apart: 6, of which 0 were waited for; matrix products, arithmetic and copies ran while one was open for 2% of the time, Pallas kernels for 24%

profile of v1, /device:TPU:1, one launch (start us, length us, event | category | flops | bytes accessed | tf_op | source)
XLA Modules:
  0.0 82.5 jit_solution(4762887114794949407)
XLA Ops:
  0.6 0.0 copy-start.1
  1.3 0.0 copy-start.7
  1.3 7.0 %vector.1 = (f32[64,2048]{1,0:T(8,128)}, f32[64,128]{1,0:T(8,128)}, f32[64,128]{1,0:T(8,128)}, f32[64,128]{1,0:T(8,128)}, f32[64,128]{1,0:T(8,128)}, /*index=5*/f32[8,32,128]{2,1,0:T(8,128)}) custom-call(f32[20]{0:T(128)} %coeffs.1, s32[16]{0:T(128)} %bitcast.15, s32[1]{0:T(128)S(6)} %copy.19.nl_count, s32[16,128]{1,0:T(8,128)} %bitcast.12, ...), custom_call_target="tpu_custom_call" | custom-call | flops 1000000000 | bytes 10485760 | tf_op jit(solution)/shard_map/vector/pallas_call | solution.py:379
  8.4 6.8 %all-to-all-start = ((f32[8,32,128]{2,1,0:T(8,128)}), f32[8,32,128]{2,1,0:T(8,128)S(1)}, u32[]{:S(2)}, u32[]{:S(2)}) async-start(f32[8,32,128]{2,1,0:T(8,128)} %get-tuple-element.12), calls=%async_computation | async-start | bytes 262144 | tf_op jit(solution)/shard_map/all_to_all | solution.py:395
  15.2 1.3 %collective-permute-start = (f32[64,128]{1,0:T(8,128)}, f32[64,128]{1,0:T(8,128)S(1)}, u32[]{:S(2)}, u32[]{:S(2)}) collective-permute-start(f32[64,128]{1,0:T(8,128)} %get-tuple-element.14), channel_id=1, source_target_pairs={{0,8},{8,16},{16,24},{24,32},{32,40},{40,48},{48,56},{56,64},{64,7... | collective-permute-start | bytes 98312 | tf_op jit(solution)/shard_map/ppermute | solution.py:397
  16.5 3.6 %collective-permute-start.1 = (f32[64,128]{1,0:T(8,128)}, f32[64,128]{1,0:T(8,128)S(1)}, u32[]{:S(2)}, u32[]{:S(2)}) collective-permute-start(f32[64,128]{1,0:T(8,128)} %get-tuple-element.15), channel_id=1, source_target_pairs={{0,120},{8,0},{16,8},{24,16},{32,24},{40,32},{48,40},{56,48},{64,5... | collective-permute-start | bytes 98312 | tf_op jit(solution)/shard_map/ppermute | solution.py:397
  20.1 1.4 %collective-permute-start.2 = (f32[64,128]{1,0:T(8,128)}, f32[64,128]{1,0:T(8,128)S(1)}, u32[]{:S(2)}, u32[]{:S(2)}) collective-permute-start(f32[64,128]{1,0:T(8,128)} %get-tuple-element.16), channel_id=1, source_target_pairs={{0,64},{8,72},{16,80},{24,88},{32,96},{40,104},{48,112},{56,120},{... | collective-permute-start | bytes 98312 | tf_op jit(solution)/shard_map/ppermute | solution.py:397
  21.5 0.0 collective-permute-start.3
  21.5 0.0 copy-done.1
  21.5 0.8 %copy.17.wave = f32[512,64]{1,0:T(8,128)} copy(f32[512,64]{0,1:T(8,128)S(1)} %copy-done.1) | data formatting | bytes 262144 | tf_op args[10]
  22.4 0.0 all-to-all-done.arrived
  22.4 0.0 copy-start.2
  22.4 0.6 copy-done.2
  23.0 2.8 %current.1 = f32[8,32,128]{2,1,0:T(8,128)} custom-call(f32[8,32,128]{2,1,0:T(8,128)} %copy-done.2, f32[512,64]{1,0:T(8,128)} %copy.17.wave, f32[1,64]{1,0:T(1,128)} %bitcast.17, bf16[6,256,256]{2,1,0:T(8,128)(2,1)} %constant.6.clone.tables), custom_call_target="tpu_custom_call" | custom-call | flops 400000000 | bytes 2000000 | tf_op jit(solution)/shard_map/current/pallas_call | solution.py:417
  25.8 5.6 %all-to-all-start.1 = ((f32[8,32,128]{2,1,0:T(8,128)}), f32[8,32,128]{2,1,0:T(8,128)S(1)}, u32[]{:S(2)}, u32[]{:S(2)}) async-start(f32[8,32,128]{2,1,0:T(8,128)} %current.1), calls=%async_computation.1 | async-start | bytes 262144 | tf_op jit(solution)/shard_map/all_to_all | solution.py:426
  31.5 9.7 %gram.1.packed_gram = f32[8,256]{1,0:T(8,128)} custom-call(f32[20,64,2048]{2,1,0:T(8,128)} %bitcast.9), custom_call_target="tpu_custom_call" | custom-call | flops 1000000000 | bytes 10485760 | tf_op jit(solution)/shard_map/gram/pallas_call | solution.py:402
  41.1 0.0 copy-done.7
  41.1 0.7 copy.18.tile_cols
  41.8 0.0 collective-permute-done.ghost_0
  41.8 0.0 copy-start.3
  41.8 0.0 collective-permute-done.1.ghost_1
  41.8 0.0 copy-start.4
  41.8 0.0 collective-permute-done.2.ghost_2
  41.9 0.0 copy-start.5
  41.9 0.0 collective-permute-done.3.ghost_3
  41.9 0.0 copy-start.6
  41.9 0.5 copy-done.3
  42.4 0.0 copy-done.4
  42.5 0.0 copy-done.5
  42.5 0.0 copy-done.6
  42.5 7.6 %coupling.1.base = f32[64,2048]{1,0:T(8,128)} custom-call(s32[16,6]{1,0:T(8,128)} %copy.18.tile_cols, f32[64,2048]{1,0:T(8,128)} %get-tuple-element.13.vector, f32[64,128]{1,0:T(8,128)} %copy-done.3, f32[64,128]{1,0:T(8,128)} %copy-done.4, f32[64,128]{1,0:T(8,128)} %copy-done.5, f32[64,128]{1,0:T(8,128)} %copy-done.6, f32[1,2048]{1,0:T(1,128)} %bitcast.13, ...), custom_call_target="tpu_custom_call" | custom-call | flops 1000000000 | bytes 6291456 | tf_op jit(solution)/shard_map/coupling/pallas_call | solution.py:431
  50.1 0.0 all-to-all-done.1.arrived
  50.1 0.0 copy-start
  50.1 0.7 copy-done
  50.7 6.2 %product.1 = (f32[64,2048]{1,0:T(8,128)}, f32[128,2,128]{2,1,0:T(2,128)}) custom-call(s32[1]{0:T(128)S(6)} %copy.19.nl_count, s32[1,512]{1,0:T(1,128)} %nl_nodes.3, f32[8,32,128]{2,1,0:T(8,128)} %copy-done, f32[64,2048]{1,0:T(8,128)} %coupling.1.base, f32[8,256]{1,0:T(8,128)} %gram.1.packed_gram, f32[20,64,2048]{2,1,0:T(8,128)} %bitcast.10), custom_call_target="tpu_custom_call" | custom-call | flops 1000000000 | bytes 10485760 | tf_op jit(solution)/shard_map/product/pallas_call | solution.py:452
  57.0 18.8 %all_to_all.15.gathered = f32[128,2,128]{2,1,0:T(2,128)} all-to-all(f32[128,2,128]{2,1,0:T(2,128)} %get-tuple-element.18), channel_id=1, replica_groups=mesh['dom_0'=4,'dom_1'=4,'harm_0'=4,'harm_1'=2] {'dom_0','dom_1','harm_0..., dimensions={0} | all-to-all | bytes 262144 | tf_op jit(solution)/shard_map/all_to_all | solution.py:466
  75.7 6.7 %residual.1 = (f32[64,2048]{1,0:T(8,128)}, f32[1,21]{1,0:T(1,128)}) custom-call(f32[128,2,128]{2,1,0:T(2,128)} %all_to_all.15.gathered, f32[2,24,256]{2,1,0:T(8,128)} %constant.7.clone.mask, bf16[2,256,128]{2,1,0:T(8,128)(2,1)} %constant.8.clone.place, f32[64,2048]{1,0:T(8,128)} %get-tuple-element.19.product, f32[20,64,2048]{2,1,0:T(8,128)} %bitcast.11), custom_call_target="tpu_custom_call" | custom-call | flops 1000000000 | bytes 10485760 | tf_op jit(solution)/shard_map/residual/pallas_call | solution.py:470
Async XLA Ops:
  0.6 20.9 %copy-start.1 = (f32[512,64]{0,1:T(8,128)S(1)}, f32[512,64]{0,1:T(8,128)}, u32[]{:S(2)}) copy-start(f32[512,64]{0,1:T(8,128)} %param.25) | copy-start | bytes 393220
  1.3 39.8 %copy-start.7 = (s32[16,6]{0,1:T(8,128)S(1)}, s32[16,6]{0,1:T(8,128)}, u32[]{:S(2)}) copy-start(s32[16,6]{0,1:T(8,128)} %param.18) | copy-start | bytes 1156
  8.4 14.0 %all-to-all-start = ((f32[8,32,128]{2,1,0:T(8,128)}), f32[8,32,128]{2,1,0:T(8,128)S(1)}, u32[]{:S(2)}, u32[]{:S(2)}) async-start(f32[8,32,128]{2,1,0:T(8,128)} %get-tuple-element.12), calls=%async_computation | async-start | bytes 262144 | tf_op jit(solution)/shard_map/all_to_all | solution.py:395
  15.2 26.6 %collective-permute-start = (f32[64,128]{1,0:T(8,128)}, f32[64,128]{1,0:T(8,128)S(1)}, u32[]{:S(2)}, u32[]{:S(2)}) collective-permute-start(f32[64,128]{1,0:T(8,128)} %get-tuple-element.14), channel_id=1, source_target_pairs={{0,8},{8,16},{16,24},{24,32},{32,40},{40,48},{48,56},{56,64},{64,7... | collective-permute-start | bytes 98312 | tf_op jit(solution)/shard_map/ppermute | solution.py:397
  16.5 25.3 %collective-permute-start.1 = (f32[64,128]{1,0:T(8,128)}, f32[64,128]{1,0:T(8,128)S(1)}, u32[]{:S(2)}, u32[]{:S(2)}) collective-permute-start(f32[64,128]{1,0:T(8,128)} %get-tuple-element.15), channel_id=1, source_target_pairs={{0,120},{8,0},{16,8},{24,16},{32,24},{40,32},{48,40},{56,48},{64,5... | collective-permute-start | bytes 98312 | tf_op jit(solution)/shard_map/ppermute | solution.py:397
  20.1 21.7 %collective-permute-start.2 = (f32[64,128]{1,0:T(8,128)}, f32[64,128]{1,0:T(8,128)S(1)}, u32[]{:S(2)}, u32[]{:S(2)}) collective-permute-start(f32[64,128]{1,0:T(8,128)} %get-tuple-element.16), channel_id=1, source_target_pairs={{0,64},{8,72},{16,80},{24,88},{32,96},{40,104},{48,112},{56,120},{... | collective-permute-start | bytes 98312 | tf_op jit(solution)/shard_map/ppermute | solution.py:397
  21.5 20.4 %collective-permute-start.3 = (f32[64,128]{1,0:T(8,128)}, f32[64,128]{1,0:T(8,128)S(1)}, u32[]{:S(2)}, u32[]{:S(2)}) collective-permute-start(f32[64,128]{1,0:T(8,128)} %get-tuple-element.17), channel_id=1, source_target_pairs={{0,72},{8,80},{16,88},{24,96},{32,104},{40,112},{48,120},{56,0},{6... | collective-permute-start | bytes 98312 | tf_op jit(solution)/shard_map/ppermute | solution.py:397
  22.4 0.6 copy-start.2
  25.8 24.3 %all-to-all-start.1 = ((f32[8,32,128]{2,1,0:T(8,128)}), f32[8,32,128]{2,1,0:T(8,128)S(1)}, u32[]{:S(2)}, u32[]{:S(2)}) async-start(f32[8,32,128]{2,1,0:T(8,128)} %current.1), calls=%async_computation.1 | async-start | bytes 262144 | tf_op jit(solution)/shard_map/all_to_all | solution.py:426
  41.8 0.6 copy-start.3
  41.8 0.6 copy-start.4
  41.9 0.6 copy-start.5
  41.9 0.6 copy-start.6
  50.1 0.7 copy-start

commit v2 on v1

--- a/solution.py
+++ b/solution.py
@@ -94,7 +94,7 @@
 
 
 def vector_kernel(coeffs, send_count, nl_count, send_nodes, nl_nodes, basis_hbm,
-                  vector, ghost_0, ghost_1, ghost_2, ghost_3, sampled,
+                  vector, ghost_0, ghost_1, ghost_2, ghost_3, sampled, cross,
                   basis, select, sems):
     start_all(basis_hbm, basis, sems)
     count, rows, nodes = basis.shape
@@ -112,6 +112,7 @@
     wanted.append(jnp.where(slot < nl_count[0], nl_nodes[...], -1))
     columns = jnp.concatenate(wanted, axis=1)
     chunk = nodes // (rows // 8)
+    cross[...] = jnp.zeros_like(cross)
 
     @pl.loop(0, rows // 8)
     def _(block):
@@ -124,51 +125,44 @@
         for j in range(1, count):
             total = total + coeffs[j] * basis[j, part, :]
         vector[part, :] = total
+        both = halves(basis[:, part, :].reshape(count * 8, nodes))
+        cross[...] += mm_nt(jnp.concatenate(both, axis=0), both[0])
 
     left = jnp.concatenate(halves(vector[...]), axis=0)
-    for peer, ghost in enumerate((ghost_0, ghost_1, ghost_2, ghost_3)):
-        taken = mm(left, select[:, peer * cap : (peer + 1) * cap])
-        ghost[...] = taken[:rows] + taken[rows:]
     half = rows // 2
     low_lanes = lax.broadcasted_iota(jnp.int32, (half, 128), 1) < 64
-    for pair in range(slots // 128):
-        first = len(PEERS) * cap + pair * 128
-        taken = mm(left, select[:, first : first + 128])
-        taken = taken[:rows] + taken[rows:]
-        top, bottom = taken[:half], taken[half:]
-        sampled[2 * pair] = jnp.where(low_lanes, top, pltpu.roll(bottom, 64, 1))
-        sampled[2 * pair + 1] = jnp.where(low_lanes, pltpu.roll(top, 64, 1), bottom)
-
-
-def gram_kernel(basis_hbm, packed, basis, sums, totals, sems):
-    start_all(basis_hbm, basis, sems)
-    count, rows, nodes = basis.shape
-    position = {pair: p for p, pair in enumerate(pair_list(count))}
-    group = 5
-    groups = [range(g, g + group) for g in range(0, count, group)]
-    sums[...] = jnp.zeros_like(sums)
-
-    @pl.loop(0, rows // 8)
-    def _(block):
-        basis_copy(basis_hbm, basis, sems, block).wait()
-        part = pl.ds(pl.multiple_of(block * 8, 8), 8)
-        for x, left in enumerate(groups):
-            for right in groups[x:]:
-                names = [(i, j) for i in left for j in right if i <= j]
-                held = {}
-                for chunk in range(nodes // 128):
-                    lanes = slice(chunk * 128, (chunk + 1) * 128)
-                    value = {i: basis[i, part, lanes] for i in set(left) | set(right)}
-                    for i, j in names:
-                        term = value[i] * value[j]
-                        held[i, j] = held[i, j] + term if chunk else term
-                for pair in names:
-                    sums[position[pair]] += held[pair]
-
-    totals[...] = jnp.zeros_like(totals)
-    for p in range(len(position)):
-        totals[p : p + 1, :] = jnp.sum(sums[p], axis=0, keepdims=True)
-    packed[...] = row_total(totals)
+    ghosts = (ghost_0, ghost_1, ghost_2, ghost_3)
+    for start in range(0, columns.shape[1], 256):
+        both = mm(left, select[:, start : start + 256])
+        both = both[:rows] + both[rows:]
+        for item, taken in enumerate((both[:, :128], both[:, 128:])):
+            item += start // 128
+            if item < len(PEERS):
+                ghosts[item][...] = taken
+                continue
+            pair = item - len(PEERS)
+            top, bottom = taken[:half], taken[half:]
+            sampled[2 * pair] = jnp.where(low_lanes, top, pltpu.roll(bottom, 64, 1))
+            sampled[2 * pair + 1] = jnp.where(low_lanes, pltpu.roll(top, 64, 1), bottom)
+
+
+def gram_line(cross, mask, place):
+    size = cross.shape[1]
+    row = lax.broadcasted_iota(jnp.int32, (size, size), 0)
+    column = lax.broadcasted_iota(jnp.int32, (size, size), 1)
+    matching = row % 8 == column % 8
+    first = jnp.where(matching, cross[:size] + cross[size:], 0.0)
+    second = jnp.where(matching, cross[size:], 0.0)
+    vector = lax.broadcasted_iota(jnp.int32, (128, size), 0)
+    owner = lax.broadcasted_iota(jnp.int32, (128, size), 1) // 8
+    select = jnp.where(vector == owner, 1.0, 0.0).astype(BF16)
+    first = sum(mm(select, part) for part in thirds(first))
+    second = sum(mm(select, part) for part in thirds(second))
+    gram = sum(mm_nt(part, select) for part in thirds(first))
+    gram = gram + sum(mm_nt(select, part) for part in thirds(second))
+    height = mask.shape[1]
+    spread = sum(mm_nt(part, place[0]) for part in thirds(gram[:height]))
+    return jnp.sum(mask[0] * spread, axis=0, keepdims=True)
 
 
 def current_kernel(arrived, wave, gain, tables, leaving):
@@ -190,7 +184,7 @@
 
     waveform = product(0, halves(even)) + product(2, halves(odd))
     gains = jnp.concatenate([gain[...], gain[...]], axis=1)
-    growth = jnp.exp(jnp.concatenate([wave[:HARM], wave[HARM:]], axis=1))
+    growth = jnp.exp(jnp.concatenate([wave[:, :HARM], wave[:, HARM:]], axis=0).T)
     current = halves(gains * growth * waveform)
     weight = jnp.where(harmonic == 0, 1.0 / SAMPLES, 2.0 / SAMPLES)
     cosine = product(0, current)
@@ -204,49 +198,50 @@
 
 
 def coupling_kernel(tile_cols, vector, ghost_0, ghost_1, ghost_2, ghost_3,
-                    self_cond, cap, tiles, base, extended):
+                    self_cond, cap, tiles_hbm, base, extended, tiles, sems):
+    tile_rows, terms = tiles.shape[:2]
+
+    def tile_copy(row):
+        return pltpu.make_async_copy(tiles_hbm.at[row], tiles.at[row], sems.at[row])
+
+    for row in range(tile_rows):
+        tile_copy(row).start()
     rows, nodes = vector.shape
     half = rows // 2
     local_tiles = nodes // 128
     peers = extended.shape[0] - local_tiles
-    step = pl.program_id(0)
     me = lax.axis_index(DOM)
-
-    @pl.when(step == 0)
-    def _():
-        for tile in range(local_tiles):
-            high, low = halves(vector[:, tile * 128 : (tile + 1) * 128])
-            extended[tile, :rows] = high
-            extended[tile, rows:] = low
-        extended[local_tiles:] = jnp.zeros((peers, 2 * rows, 128), BF16)
-        for jump, ghost in zip(PEERS, (ghost_0, ghost_1, ghost_2, ghost_3)):
-            sender = local_tiles + lax.rem(me + peers - jump, peers)
-            high, low = halves(ghost[...])
-            extended[sender, :rows] = high
-            extended[sender, rows:] = low
-
-    per_step, terms = tiles.shape[0], tiles.shape[1]
+    for tile in range(local_tiles):
+        high, low = halves(vector[:, tile * 128 : (tile + 1) * 128])
+        extended[tile, :rows] = high
+        extended[tile, rows:] = low
+    extended[local_tiles:] = jnp.zeros((peers, 2 * rows, 128), BF16)
+    for jump, ghost in zip(PEERS, (ghost_0, ghost_1, ghost_2, ghost_3)):
+        sender = local_tiles + lax.rem(me + peers - jump, peers)
+        high, low = halves(ghost[...])
+        extended[sender, :rows] = high
+        extended[sender, rows:] = low
+
     first = lax.axis_index(HARM_AXES) * half
     harmonic = first + lax.broadcasted_iota(jnp.int32, (half, 128), 0)
     angular = (2.0 * math.pi / HARM) * harmonic.astype(F32)
-    for t in range(per_step):
-        row = step * per_step + t
-        total = jnp.zeros((rows, 128), F32)
-        for i in range(0, terms, 2):
-            left = jnp.concatenate(
-                [extended[tile_cols[row, i]], extended[tile_cols[row, i + 1]]], axis=1
-            )
-            high, low = halves(tiles[t, i : i + 2].reshape(256, 128))
-            main = mm(left, high)
-            total = total + main[:rows] + main[rows:] + mm(left[:rows], low)
+
+    def one_row(row):
+        tile_copy(row).wait()
+        left = jnp.concatenate([extended[tile_cols[i, row]] for i in range(terms)], axis=1)
+        right = jnp.concatenate(halves(tiles[row].reshape(terms * 128, 128)), axis=1)
+        total = mm(left, right)
+        total = total[:rows, :128] + total[rows:, :128] + total[:rows, 128:]
         lanes = pl.ds(pl.multiple_of(row * 128, 128), 128)
         cosine, sine = vector[:half, lanes], vector[half:, lanes]
         ground, reactive = self_cond[:, lanes], angular * cap[:, lanes]
         base[:half, lanes] = total[:half] + ground * cosine - reactive * sine
         base[half:, lanes] = total[half:] + ground * sine + reactive * cosine
 
-
-def product_kernel(nl_count, nl_nodes, arrived, base, packed_gram, basis_hbm,
+    pl.loop(0, tile_rows)(one_row)
+
+
+def product_kernel(nl_count, nl_nodes, arrived, base, cross, mask, place, basis_hbm,
                    product, packed, basis, totals, sems):
     start_all(basis_hbm, basis, sems)
     count, rows, nodes = basis.shape
@@ -291,14 +286,13 @@
     first = count * (count + 1) // 2
     for a in range(count + 1):
         totals[first + a : first + a + 1, :] = jnp.sum(sums[a], axis=0, keepdims=True)
-    line = (row_total(totals) + packed_gram[...])[:1]
+    line = row_total(totals)[:1] + gram_line(cross, mask, place)
     both = jnp.concatenate([line[:, :128], line[:, 128:]], axis=0)
     packed[...] = jnp.broadcast_to(both[None], packed.shape)
 
 
-def residual_kernel(entries, gathered, mask, place, product, basis_hbm,
-                    residual, column, basis, weights, sems):
-    start_all(basis_hbm, basis, sems)
+def residual_kernel(entries, gathered, mask, place, product, basis,
+                    residual, column, weights):
     count, rows, nodes = basis.shape
     height = mask.shape[1]
     scale = 1.0 / entries
@@ -333,7 +327,6 @@
 
     @pl.loop(0, rows // 8)
     def _(block):
-        basis_copy(basis_hbm, basis, sems, block).wait()
         part = pl.ds(pl.multiple_of(block * 8, 8), 8)
         hess = [jnp.broadcast_to(weights[a : a + 1, :], (8, 128)) for a in range(count)]
         for chunk in range(nodes // 128):
@@ -342,6 +335,10 @@
             while len(terms) > 1:
                 terms = [sum(terms[i : i + 2]) for i in range(0, len(terms), 2)]
             residual[part, lanes] = (product[part, lanes] - terms[0]) * inverse
+
+
+def in_hbm(value):
+    return pltpu.with_memory_space_constraint(value, pltpu.HBM)
 
 
 def local(
@@ -369,28 +366,32 @@
     vmem = pl.BlockSpec(memory_space=pltpu.VMEM)
     hbm = pl.BlockSpec(memory_space=pl.ANY)
     shape = jax.ShapeDtypeStruct
-    basis_scratch = pltpu.VMEM((count, rows, nodes), F32)
-    sems = pltpu.SemaphoreType.DMA((rows // 8,))
+    params = pltpu.CompilerParams(vmem_limit_bytes=24 * 2**20)
     basis_bytes = 4 * count * rows * nodes
 
     def cost(flops, size):
         return pl.CostEstimate(flops=flops, bytes_accessed=size, transcendentals=0)
 
-    vector, *ghosts, sampled = pl.pallas_call(
+    vector, *ghosts, sampled, cross = pl.pallas_call(
         vector_kernel,
         out_shape=[shape((rows, nodes), F32)]
         + [shape((rows, peer_cap), F32)] * len(PEERS)
-        + [shape((groups, harm_local, 128), F32)],
+        + [shape((groups, harm_local, 128), F32)]
+        + [shape((count * 16, count * 8), F32)],
         in_specs=[smem, smem, smem, vmem, vmem, hbm],
-        out_specs=[vmem] * (2 + len(PEERS)),
+        out_specs=[vmem] * (3 + len(PEERS)),
         scratch_shapes=[
-            basis_scratch,
+            pltpu.VMEM((count, rows, nodes), F32),
             pltpu.VMEM((nodes, len(PEERS) * peer_cap + nl_cap), BF16),
-            sems,
+            pltpu.SemaphoreType.DMA((rows // 8,)),
         ],
+        compiler_params=params,
         cost_estimate=cost(10**9, basis_bytes),
         name="vector",
-    )(coeffs, send_count[0], nl_count, send_nodes[0], nl_nodes, basis)
+    )(
+        in_hbm(coeffs), in_hbm(send_count[0]), nl_count,
+        in_hbm(send_nodes[0]), in_hbm(nl_nodes), in_hbm(basis),
+    )
 
     arrived_spectrum = lax.all_to_all(sampled, HARM_AXES, 0, 0, tiled=True)
     ghosts = [
@@ -398,84 +399,74 @@
         for jump, ghost in zip(PEERS, ghosts)
     ]
 
-    width = 256
-    packed_gram = pl.pallas_call(
-        gram_kernel,
-        out_shape=shape((8, width), F32),
-        in_specs=[hbm],
-        out_specs=vmem,
-        scratch_shapes=[
-            basis_scratch,
-            pltpu.VMEM((count * (count + 1) // 2, 8, 128), F32),
-            pltpu.VMEM((width, 128), F32),
-            sems,
-        ],
-        cost_estimate=cost(10**9, basis_bytes),
-        name="gram",
-    )(basis)
-
     leaving = pl.pallas_call(
         current_kernel,
         out_shape=shape((groups, harm_local, 128), F32),
         in_specs=[vmem] * 4,
         out_specs=vmem,
+        compiler_params=params,
         cost_estimate=cost(4 * 10**8, 2 * 10**6),
         name="current",
-    )(arrived_spectrum, op_wave, nl_gain.reshape(1, -1), jnp.asarray(transform_tables()))
+    )(arrived_spectrum, op_wave.T, nl_gain.reshape(1, -1), jnp.asarray(transform_tables()))
 
     returned = lax.all_to_all(leaving, HARM_AXES, 0, 0, tiled=True)
 
     tile_rows, terms = tile_cols.shape
-    per_step = 2
-    whole = lambda *dims: pl.BlockSpec(dims, lambda i: (0,) * len(dims))
     base = pl.pallas_call(
         coupling_kernel,
-        grid=(tile_rows // per_step,),
         out_shape=shape((rows, nodes), F32),
-        in_specs=[smem, whole(rows, nodes)]
-        + [whole(rows, peer_cap)] * len(PEERS)
-        + [
-            whole(1, nodes),
-            whole(1, nodes),
-            pl.BlockSpec((per_step, terms, 128, 128), lambda i: (i, 0, 0, 0)),
+        in_specs=[smem] + [vmem] * (3 + len(PEERS)) + [hbm],
+        out_specs=vmem,
+        scratch_shapes=[
+            pltpu.VMEM((nodes // 128 + peers, 2 * rows, 128), BF16),
+            pltpu.VMEM(conductance_tiles.shape, F32),
+            pltpu.SemaphoreType.DMA((tile_rows,)),
         ],
-        out_specs=whole(rows, nodes),
-        scratch_shapes=[pltpu.VMEM((nodes // 128 + peers, 2 * rows, 128), BF16)],
+        compiler_params=params,
         cost_estimate=cost(10**9, 4 * tile_rows * terms * 128 * 128),
         name="coupling",
     )(
-        tile_cols, vector, *ghosts, self_cond.reshape(1, -1), cap.reshape(1, -1),
-        conductance_tiles,
+        tile_cols.T, vector, *ghosts, self_cond.reshape(1, -1), cap.reshape(1, -1),
+        in_hbm(conductance_tiles),
     )
 
     devices = peers * groups
-    product, packed = pl.pallas_call(
+    width = 256
+    mask, place = unpack_tables(count, 24, width)
+    mask, place = jnp.asarray(mask), jnp.asarray(place)
+    product, packed, held = pl.pallas_call(
         product_kernel,
-        out_shape=[shape((rows, nodes), F32), shape((devices, width // 128, 128), F32)],
-        in_specs=[smem, vmem, vmem, vmem, vmem, hbm],
-        out_specs=[vmem, vmem],
+        out_shape=[
+            shape((rows, nodes), F32),
+            shape((devices, width // 128, 128), F32),
+            pltpu.VMEM((count, rows, nodes), F32),
+        ],
+        in_specs=[smem] + [vmem] * 6 + [hbm],
+        out_specs=[vmem] * 3,
         scratch_shapes=[
-            basis_scratch,
             pltpu.VMEM((width, 128), F32),
-            sems,
+            pltpu.SemaphoreType.DMA((rows // 8,)),
         ],
+        compiler_params=params,
         cost_estimate=cost(10**9, basis_bytes),
         name="product",
-    )(nl_count, nl_nodes, returned, base, packed_gram, basis)
+    )(nl_count, nl_nodes, returned, base, cross, mask, place, in_hbm(basis))
 
     gathered = lax.all_to_all(packed, DOM_HARM, 0, 0, tiled=True)
 
     entries = rows * groups * nodes * peers
-    mask, place = unpack_tables(count, 24, width)
     residual, column = pl.pallas_call(
         functools.partial(residual_kernel, float(entries)),
         out_shape=[shape((rows, nodes), F32), shape((1, count + 1), F32)],
-        in_specs=[vmem, vmem, vmem, vmem, hbm],
+        in_specs=[vmem] * 5,
         out_specs=[vmem, vmem],
-        scratch_shapes=[basis_scratch, pltpu.VMEM((24, 128), F32), sems],
+        scratch_shapes=[pltpu.VMEM((24, 128), F32)],
+        compiler_params=params,
         cost_estimate=cost(10**9, basis_bytes),
         name="residual",
-    )(gathered, jnp.asarray(mask), jnp.asarray(place), product, basis)
+    )(
+        gathered, mask, place, product, pltpu.with_memory_space_constraint(held, pltpu.VMEM)
+    )
     return (residual.reshape(2, harm_local, nodes), column.reshape(count + 1))
 
 

time: 83 us -> 64 us (0.77)
  Pallas kernels: 40 us -> 24.8 us
  local copies, waits for them, and re-layouts: 3.44 us -> 0.05 us
    pallas_call x2 -> x1, Pallas kernels: 17.3 us -> 5.37 us  [local(): pl.pallas_call(coupling_kernel, out_shape=shape((rows, nodes), F32), in_s...]
    unnamed x18, local copies, waits for them, and re-layouts: 3.44 us -> 0.05 us
    pallas_call x1, Pallas kernels: 6.73 us -> 3.83 us  [local(): pl.pallas_call(functools.partial(residual_kernel, float(entries)), out_sh...]
    pallas_call x1, Pallas kernels: 7.04 us -> 9.06 us  [local(): pl.pallas_call(vector_kernel, out_shape=[shape((rows, nodes), F32)] + [sh...]
    pallas_call x1, Pallas kernels: 2.8 us -> 1.52 us  [local(): pl.pallas_call(current_kernel, out_shape=shape((groups, harm_local, 128),...]
    pallas_call x1, Pallas kernels: 6.23 us -> 5.04 us  [local(): pl.pallas_call(product_kernel, out_shape=[shape((rows, nodes), F32), shap...]
  transfers between devices with their start and end apart: 6 -> 6, of which waited for: 0 -> 0; matrix products, arithmetic and copies ran while one was open for 2% -> 0% of each run, Pallas kernels for 24% -> 11%
where the time goes in v2:
time: 64 us; the launch traced here: 63.6 us
  Pallas kernels  24.8 us (39%)
  starting transfers between devices  18.8 us (29%)
  blocking collectives  18.4 us (29%)
  between operations  1.55 us (2%)
    all_to_all x1, blocking collectives, local(): gathered = lax.all_to_all(packed, DOM_HARM, 0, 0, tiled=True)  18.4 us
    pallas_call x1, Pallas kernels, local(): pl.pallas_call(vector_kernel, out_shape=[shape((rows, nodes), F32)] + [sh...  9.06 us
    all_to_all x1, starting transfers between devices, local(): arrived_spectrum = lax.all_to_all(sampled, HARM_AXES, 0, 0, tiled=True)  6.8 us
    ppermute x4, starting transfers between devices, local(): lax.ppermute(ghost, DOM, [(i, (i + jump) % peers) for i in range(peers)])  6.33 us
    all_to_all x1, starting transfers between devices, local(): returned = lax.all_to_all(leaving, HARM_AXES, 0, 0, tiled=True)  5.64 us
    pallas_call x1, Pallas kernels, local(): pl.pallas_call(coupling_kernel, out_shape=shape((rows, nodes), F32), in_s...  5.37 us
    pallas_call x1, Pallas kernels, local(): pl.pallas_call(product_kernel, out_shape=[shape((rows, nodes), F32), shap...  5.04 us
    pallas_call x1, Pallas kernels, local(): pl.pallas_call(functools.partial(residual_kernel, float(entries)), out_sh...  3.83 us
  transfers between devices with their start and end apart: 6, of which 0 were waited for; matrix products, arithmetic and copies ran while one was open for 0% of the time, Pallas kernels for 11%

profile of v2, /device:TPU:1, one launch (start us, length us, event | category | flops | bytes accessed | tf_op | source)
XLA Modules:
  0.0 63.6 jit_solution(9200673718944550466)
XLA Ops:
  0.6 0.0 copy-start.8
  0.6 0.0 copy-start
  0.7 0.0 copy-start.1
  0.7 0.0 copy-start.4
  0.7 0.0 copy-start.7
  0.7 0.0 copy-start.6
  0.7 0.0 copy-start.3
  0.7 0.0 copy-start.2
  0.7 0.0 copy-start.5
  1.4 9.1 %vector.1 = (f32[64,2048]{1,0:T(8,128)S(1)}, f32[64,128]{1,0:T(8,128)S(1)}, f32[64,128]{1,0:T(8,128)S(1)}, f32[64,128]{1,0:T(8,128)S(1)}, f32[64,128]{1,0:T(8,12...) custom-call(f32[20]{0:T(128)} %coeffs.1, s32[16]{0:T(128)} %bitcast.18, s32[1]{0:T(128)S(6)} %copy.17.nl_count, ...), custom_call_target="tpu_custom_call" | custom-call | flops 1000000000 | bytes 10485760 | tf_op jit(solution)/shard_map/vector/pallas_call | solution.py:375
  10.5 6.8 %all-to-all-start = ((f32[8,32,128]{2,1,0:T(8,128)}), f32[8,32,128]{2,1,0:T(8,128)S(1)}, u32[]{:S(2)}, u32[]{:S(2)}) async-start(f32[8,32,128]{2,1,0:T(8,128)} %get-tuple-element.14), calls=%async_computation | async-start | bytes 262144 | tf_op jit(solution)/shard_map/all_to_all | solution.py:396
  17.3 1.3 %collective-permute-start = (f32[64,128]{1,0:T(8,128)S(1)}, f32[64,128]{1,0:T(8,128)S(1)}, u32[]{:S(2)}, u32[]{:S(2)}) collective-permute-start(f32[64,128]{1,0:T(8,128)S(1)} %get-tuple-element.16), channel_id=1, source_target_pairs={{0,8},{8,16},{16,24},{24,32},{32,40},{40,48},{48,56},{56,64},{64,7... | collective-permute-start | bytes 98312 | tf_op jit(solution)/shard_map/ppermute | solution.py:398
  18.6 3.7 %collective-permute-start.1 = (f32[64,128]{1,0:T(8,128)S(1)}, f32[64,128]{1,0:T(8,128)S(1)}, u32[]{:S(2)}, u32[]{:S(2)}) collective-permute-start(f32[64,128]{1,0:T(8,128)S(1)} %get-tuple-element.17), channel_id=1, source_target_pairs={{0,120},{8,0},{16,8},{24,16},{32,24},{40,32},{48,40},{56,48},{64,5... | collective-permute-start | bytes 98312 | tf_op jit(solution)/shard_map/ppermute | solution.py:398
  22.3 1.4 %collective-permute-start.2 = (f32[64,128]{1,0:T(8,128)S(1)}, f32[64,128]{1,0:T(8,128)S(1)}, u32[]{:S(2)}, u32[]{:S(2)}) collective-permute-start(f32[64,128]{1,0:T(8,128)S(1)} %get-tuple-element.18), channel_id=1, source_target_pairs={{0,64},{8,72},{16,80},{24,88},{32,96},{40,104},{48,112},{56,120},{... | collective-permute-start | bytes 98312 | tf_op jit(solution)/shard_map/ppermute | solution.py:398
  23.6 0.0 collective-permute-start.3
  23.7 0.0 all-to-all-done.arrived
  23.7 0.0 copy-done.8
  23.7 0.0 copy-done.7
  23.7 0.0 copy-done.6
  23.7 1.5 %current.1 = f32[8,32,128]{2,1,0:T(8,128)} custom-call(f32[8,32,128]{2,1,0:T(8,128)S(1)} %all-to-all-done.arrived, f32[64,512]{1,0:T(8,128)S(1)} %bitcast.13, f32[1,64]{1,0:T(1,128)S(1)} %bitcast.14, bf16[6,256,256]{2,1,0:T(8,128)(2,1)S(1)} %copy-done.8), custom_call_target="tpu_custom_call" | custom-call | flops 400000000 | bytes 2000000 | tf_op jit(solution)/shard_map/current/pallas_call | solution.py:402
  25.2 5.6 %all-to-all-start.1 = ((f32[8,32,128]{2,1,0:T(8,128)}), f32[8,32,128]{2,1,0:T(8,128)S(1)}, u32[]{:S(2)}, u32[]{:S(2)}) async-start(f32[8,32,128]{2,1,0:T(8,128)} %current.1), calls=%async_computation.1 | async-start | bytes 262144 | tf_op jit(solution)/shard_map/all_to_all | solution.py:412
  30.8 0.0 collective-permute-done.ghost_0
  30.8 0.0 collective-permute-done.1.ghost_1
  30.9 0.0 collective-permute-done.2.ghost_2
  30.9 0.0 collective-permute-done.3.ghost_3
  30.9 0.0 copy-done.3
  30.9 0.0 copy-done.2
  30.9 0.0 copy-done.5
  30.9 5.4 %coupling.1.base = f32[64,2048]{1,0:T(8,128)S(1)} custom-call(s32[6,16]{1,0:T(8,128)S(1)} %bitcast.12, f32[64,2048]{1,0:T(8,128)S(1)} %get-tuple-element.15.vector, f32[64,128]{1,0:T(8,128)S(1)} %collective-permute-done.ghost_0, f32[64,128]{1,0:T(8,128)S(1)} %collective-permute-done.1.ghost_1, f32[64,128]{1,0:T(8,128)S(1)} %collective-permute-done.2.ghost_2, ...), custom_call_target="tpu_custom_call" | custom-call | flops 1000000000 | bytes 6291456 | tf_op jit(solution)/shard_map/coupling/pallas_call | solution.py:415
  36.3 0.0 all-to-all-done.1.arrived
  36.3 0.0 copy-done
  36.3 0.0 copy-done.1
  36.3 0.0 copy-done.4
  36.3 5.0 %product.1 = (f32[64,2048]{1,0:T(8,128)S(1)}, f32[128,2,128]{2,1,0:T(2,128)S(1)}, f32[20,64,2048]{2,1,0:T(8,128)S(1)}) custom-call(s32[1]{0:T(128)S(6)} %copy.17.nl_count, s32[1,512]{1,0:T(1,128)S(1)} %copy-done.4, f32[8,32,128]{2,1,0:T(8,128)S(1)} %all-to-all-done.1.arrived, f32[64,2048]{1,0:T(8,128)S(1)} %coupling.1.base, ...), custom_call_target="tpu_custom_call" | custom-call | flops 1000000000 | bytes 10485760 | tf_op jit(solution)/shard_map/product/pallas_call | solution.py:437
  41.4 18.4 %all_to_all.15.gathered = f32[128,2,128]{2,1,0:T(2,128)S(1)} all-to-all(f32[128,2,128]{2,1,0:T(2,128)S(1)} %get-tuple-element.21), channel_id=1, replica_groups=mesh['dom_0'=4,'dom_1'=4,'harm_0'=4,'harm_1'=2] {'dom_0','dom_1','harm_0..., dimensions={0} | all-to-all | bytes 262144 | tf_op jit(solution)/shard_map/all_to_all | solution.py:455
  59.7 3.8 %residual.1 = (f32[64,2048]{1,0:T(8,128)}, f32[1,21]{1,0:T(1,128)}) custom-call(f32[128,2,128]{2,1,0:T(2,128)S(1)} %all_to_all.15.gathered, f32[2,24,256]{2,1,0:T(8,128)S(1)} %copy-done.1, bf16[2,256,128]{2,1,0:T(8,128)(2,1)S(1)} %copy-done, f32[64,2048]{1,0:T(8,128)S(1)} %get-tuple-element.22.product, f32[20,64,2048]{2,1,0:T(8,128)S(1)} %get-tuple-element.23.basis), custom_call_target="tpu_custom_call" | custom-call | flops 1000000000 | bytes 10485760 | tf_op jit(solution)/shard_map/residual/pallas_call | solution.py:458
Async XLA Ops:
  0.6 23.0 %copy-start.8 = (bf16[6,256,256]{2,1,0:T(8,128)(2,1)S(1)}, bf16[6,256,256]{2,1,0:T(8,128)(2,1)}, u32[]{:S(2)}) copy-start(bf16[6,256,256]{2,1,0:T(8,128)(2,1)} %constant.6.clone.tables) | copy-start | bytes 2359300
  0.6 35.6 %copy-start = (bf16[2,256,128]{2,1,0:T(8,128)(2,1)S(1)}, bf16[2,256,128]{2,1,0:T(8,128)(2,1)}, u32[]{:S(2)}) copy-start(bf16[2,256,128]{2,1,0:T(8,128)(2,1)} %constant.8.clone.place) | copy-start | bytes 393220
  0.7 35.6 %copy-start.1 = (f32[2,24,256]{2,1,0:T(8,128)S(1)}, f32[2,24,256]{2,1,0:T(8,128)}, u32[]{:S(2)}) copy-start(f32[2,24,256]{2,1,0:T(8,128)} %constant.7.clone.mask) | copy-start | bytes 147460
  0.7 35.6 %copy-start.4 = (s32[1,512]{1,0:T(1,128)S(1)}, s32[1,512]{1,0:T(1,128)}, u32[]{:S(2)}) copy-start(s32[1,512]{1,0:T(1,128)} %nl_nodes.3) | copy-start | bytes 6148
  0.7 23.0 %copy-start.7 = (f32[64]{0:T(128)S(1)}, f32[64]{0:T(128)}, u32[]{:S(2)}) copy-start(f32[64]{0:T(128)} %param.26) | copy-start | bytes 772
  0.7 23.0 %copy-start.6 = (f32[512,64]{0,1:T(8,128)S(1)}, f32[512,64]{0,1:T(8,128)}, u32[]{:S(2)}) copy-start(f32[512,64]{0,1:T(8,128)} %param.25) | copy-start | bytes 393220
  0.7 30.2 %copy-start.3 = (f32[2048]{0:T(1024)S(1)}, f32[2048]{0:T(1024)}, u32[]{:S(2)}) copy-start(f32[2048]{0:T(1024)} %param.20) | copy-start | bytes 24580
  0.7 30.2 %copy-start.2 = (f32[2048]{0:T(1024)S(1)}, f32[2048]{0:T(1024)}, u32[]{:S(2)}) copy-start(f32[2048]{0:T(1024)} %param.19) | copy-start | bytes 24580
  0.7 30.2 %copy-start.5 = (s32[16,6]{0,1:T(8,128)S(1)}, s32[16,6]{0,1:T(8,128)}, u32[]{:S(2)}) copy-start(s32[16,6]{0,1:T(8,128)} %param.18) | copy-start | bytes 1156
  10.5 13.1 %all-to-all-start = ((f32[8,32,128]{2,1,0:T(8,128)}), f32[8,32,128]{2,1,0:T(8,128)S(1)}, u32[]{:S(2)}, u32[]{:S(2)}) async-start(f32[8,32,128]{2,1,0:T(8,128)} %get-tuple-element.14), calls=%async_computation | async-start | bytes 262144 | tf_op jit(solution)/shard_map/all_to_all | solution.py:396
  17.3 13.5 %collective-permute-start = (f32[64,128]{1,0:T(8,128)S(1)}, f32[64,128]{1,0:T(8,128)S(1)}, u32[]{:S(2)}, u32[]{:S(2)}) collective-permute-start(f32[64,128]{1,0:T(8,128)S(1)} %get-tuple-element.16), channel_id=1, source_target_pairs={{0,8},{8,16},{16,24},{24,32},{32,40},{40,48},{48,56},{56,64},{64,7... | collective-permute-start | bytes 98312 | tf_op jit(solution)/shard_map/ppermute | solution.py:398
  18.6 12.2 %collective-permute-start.1 = (f32[64,128]{1,0:T(8,128)S(1)}, f32[64,128]{1,0:T(8,128)S(1)}, u32[]{:S(2)}, u32[]{:S(2)}) collective-permute-start(f32[64,128]{1,0:T(8,128)S(1)} %get-tuple-element.17), channel_id=1, source_target_pairs={{0,120},{8,0},{16,8},{24,16},{32,24},{40,32},{48,40},{56,48},{64,5... | collective-permute-start | bytes 98312 | tf_op jit(solution)/shard_map/ppermute | solution.py:398
  22.3 8.6 %collective-permute-start.2 = (f32[64,128]{1,0:T(8,128)S(1)}, f32[64,128]{1,0:T(8,128)S(1)}, u32[]{:S(2)}, u32[]{:S(2)}) collective-permute-start(f32[64,128]{1,0:T(8,128)S(1)} %get-tuple-element.18), channel_id=1, source_target_pairs={{0,64},{8,72},{16,80},{24,88},{32,96},{40,104},{48,112},{56,120},{... | collective-permute-start | bytes 98312 | tf_op jit(solution)/shard_map/ppermute | solution.py:398
  23.6 7.2 %collective-permute-start.3 = (f32[64,128]{1,0:T(8,128)S(1)}, f32[64,128]{1,0:T(8,128)S(1)}, u32[]{:S(2)}, u32[]{:S(2)}) collective-permute-start(f32[64,128]{1,0:T(8,128)S(1)} %get-tuple-element.19), channel_id=1, source_target_pairs={{0,72},{8,80},{16,88},{24,96},{32,104},{40,112},{48,120},{56,0},{6... | collective-permute-start | bytes 98312 | tf_op jit(solution)/shard_map/ppermute | solution.py:398
  25.2 11.1 %all-to-all-start.1 = ((f32[8,32,128]{2,1,0:T(8,128)}), f32[8,32,128]{2,1,0:T(8,128)S(1)}, u32[]{:S(2)}, u32[]{:S(2)}) async-start(f32[8,32,128]{2,1,0:T(8,128)} %current.1), calls=%async_computation.1 | async-start | bytes 262144 | tf_op jit(solution)/shard_map/all_to_all | solution.py:412

commit v3 on v2

--- a/solution.py
+++ b/solution.py
@@ -109,16 +109,18 @@
         listed = send_nodes[pl.ds(peer, 1), :]
         wanted.append(jnp.where(lane < send_count[peer], listed, -1))
     slot = lax.broadcasted_iota(jnp.int32, (1, slots), 1)
-    wanted.append(jnp.where(slot < nl_count[0], nl_nodes[...], -1))
+    wanted.append(jnp.where(slot < nl_count[...], nl_nodes[...], -1))
     columns = jnp.concatenate(wanted, axis=1)
-    chunk = nodes // (rows // 8)
     cross[...] = jnp.zeros_like(cross)
+
+    @pl.loop(0, nodes // 128)
+    def _(block):
+        start = pl.multiple_of(block * 128, 128)
+        node = lax.broadcasted_iota(jnp.int32, (128, columns.shape[1]), 0) + start
+        select[pl.ds(start, 128), :] = jnp.where(node == columns, 1.0, 0.0).astype(BF16)
 
     @pl.loop(0, rows // 8)
     def _(block):
-        start = pl.multiple_of(block * chunk, chunk)
-        node = lax.broadcasted_iota(jnp.int32, (chunk, columns.shape[1]), 0) + start
-        select[pl.ds(start, chunk), :] = jnp.where(node == columns, 1.0, 0.0).astype(BF16)
         basis_copy(basis_hbm, basis, sems, block).wait()
         part = pl.ds(pl.multiple_of(block * 8, 8), 8)
         total = coeffs[0] * basis[0, part, :]
@@ -198,7 +200,8 @@
 
 
 def coupling_kernel(tile_cols, vector, ghost_0, ghost_1, ghost_2, ghost_3,
-                    self_cond, cap, tiles_hbm, base, extended, tiles, sems):
+                    self_cond, cap, cross, mask, place, tiles_hbm, base, packed_gram,
+                    extended, tiles, live, order, sems):
     tile_rows, terms = tiles.shape[:2]
 
     def tile_copy(row):
@@ -216,8 +219,11 @@
         extended[tile, :rows] = high
         extended[tile, rows:] = low
     extended[local_tiles:] = jnp.zeros((peers, 2 * rows, 128), BF16)
+    for tile in range(local_tiles + peers):
+        live[tile] = jnp.int32(tile < local_tiles)
     for jump, ghost in zip(PEERS, (ghost_0, ghost_1, ghost_2, ghost_3)):
         sender = local_tiles + lax.rem(me + peers - jump, peers)
+        live[sender] = jnp.int32(1)
         high, low = halves(ghost[...])
         extended[sender, :rows] = high
         extended[sender, rows:] = low
@@ -226,11 +232,22 @@
     harmonic = first + lax.broadcasted_iota(jnp.int32, (half, 128), 0)
     angular = (2.0 * math.pi / HARM) * harmonic.astype(F32)
 
-    def one_row(row):
-        tile_copy(row).wait()
-        left = jnp.concatenate([extended[tile_cols[i, row]] for i in range(terms)], axis=1)
-        right = jnp.concatenate(halves(tiles[row].reshape(terms * 128, 128)), axis=1)
-        total = mm(left, right)
+    packed_gram[...] = gram_line(cross, mask, place)
+
+    def live_first(row, slot):
+        flags = [live[tile_cols[i, row]] for i in range(terms)]
+        front, back = jnp.int32(0), sum(flags)
+        number = back
+        for i, flag in enumerate(flags):
+            order[slot, jnp.where(flag == 1, front, back)] = jnp.int32(i)
+            front, back = front + flag, back + 1 - flag
+        return number
+
+    def one_row(row, slot, width):
+        picks = [order[slot, i] for i in range(width)]
+        left = jnp.concatenate([extended[tile_cols[i, row]] for i in picks], axis=1)
+        right = jnp.concatenate([tiles[row, i] for i in picks], axis=0)
+        total = mm(left, jnp.concatenate(halves(right), axis=1))
         total = total[:rows, :128] + total[rows:, :128] + total[:rows, 128:]
         lanes = pl.ds(pl.multiple_of(row * 128, 128), 128)
         cosine, sine = vector[:half, lanes], vector[half:, lanes]
@@ -238,17 +255,31 @@
         base[:half, lanes] = total[:half] + ground * cosine - reactive * sine
         base[half:, lanes] = total[half:] + ground * sine + reactive * cosine
 
-    pl.loop(0, tile_rows)(one_row)
-
-
-def product_kernel(nl_count, nl_nodes, arrived, base, cross, mask, place, basis_hbm,
+    together = 2
+
+    @pl.loop(0, tile_rows, step=together)
+    def _(first_row):
+        needed = jnp.int32(0)
+        for slot in range(together):
+            tile_copy(first_row + slot).wait()
+            needed = jnp.maximum(needed, live_first(first_row + slot, slot))
+        for width in range(2, terms + 1, 2):
+            fits = needed <= width if width < terms else needed >= 0
+
+            @pl.when(fits & (needed > width - 2) if width > 2 else fits)
+            def _(width=width):
+                for slot in range(together):
+                    one_row(first_row + slot, slot, width)
+
+
+def product_kernel(nl_count, nl_nodes, arrived, base, packed_gram, basis_hbm,
                    product, packed, basis, totals, sems):
     start_all(basis_hbm, basis, sems)
     count, rows, nodes = basis.shape
     half = rows // 2
     slots = nl_nodes.shape[1]
     slot = lax.broadcasted_iota(jnp.int32, (1, slots), 1)
-    columns = jnp.where(slot < nl_count[0], nl_nodes[...], -1)
+    columns = jnp.where(slot < nl_count[...], nl_nodes[...], -1)
     low_lanes = lax.broadcasted_iota(jnp.int32, (half, 128), 1) < 64
     top, bottom = [], []
     for pair in range(slots // 128):
@@ -286,7 +317,7 @@
     first = count * (count + 1) // 2
     for a in range(count + 1):
         totals[first + a : first + a + 1, :] = jnp.sum(sums[a], axis=0, keepdims=True)
-    line = row_total(totals)[:1] + gram_line(cross, mask, place)
+    line = row_total(totals)[:1] + packed_gram[...]
     both = jnp.concatenate([line[:, :128], line[:, 128:]], axis=0)
     packed[...] = jnp.broadcast_to(both[None], packed.shape)
 
@@ -378,7 +409,7 @@
         + [shape((rows, peer_cap), F32)] * len(PEERS)
         + [shape((groups, harm_local, 128), F32)]
         + [shape((count * 16, count * 8), F32)],
-        in_specs=[smem, smem, smem, vmem, vmem, hbm],
+        in_specs=[smem, smem, vmem, vmem, vmem, hbm],
         out_specs=[vmem] * (3 + len(PEERS)),
         scratch_shapes=[
             pltpu.VMEM((count, rows, nodes), F32),
@@ -389,7 +420,7 @@
         cost_estimate=cost(10**9, basis_bytes),
         name="vector",
     )(
-        in_hbm(coeffs), in_hbm(send_count[0]), nl_count,
+        in_hbm(coeffs), in_hbm(send_count[0]), nl_count.reshape(1, 1),
         in_hbm(send_nodes[0]), in_hbm(nl_nodes), in_hbm(basis),
     )
 
@@ -412,14 +443,19 @@
     returned = lax.all_to_all(leaving, HARM_AXES, 0, 0, tiled=True)
 
     tile_rows, terms = tile_cols.shape
-    base = pl.pallas_call(
+    width = 256
+    mask, place = unpack_tables(count, 24, width)
+    mask, place = jnp.asarray(mask), jnp.asarray(place)
+    base, packed_gram = pl.pallas_call(
         coupling_kernel,
-        out_shape=shape((rows, nodes), F32),
-        in_specs=[smem] + [vmem] * (3 + len(PEERS)) + [hbm],
-        out_specs=vmem,
+        out_shape=[shape((rows, nodes), F32), shape((1, width), F32)],
+        in_specs=[smem] + [vmem] * (6 + len(PEERS)) + [hbm],
+        out_specs=[vmem] * 2,
         scratch_shapes=[
             pltpu.VMEM((nodes // 128 + peers, 2 * rows, 128), BF16),
             pltpu.VMEM(conductance_tiles.shape, F32),
+            pltpu.SMEM((nodes // 128 + peers,), jnp.int32),
+            pltpu.SMEM((2, terms), jnp.int32),
             pltpu.SemaphoreType.DMA((tile_rows,)),
         ],
         compiler_params=params,
@@ -427,13 +463,10 @@
         name="coupling",
     )(
         tile_cols.T, vector, *ghosts, self_cond.reshape(1, -1), cap.reshape(1, -1),
-        in_hbm(conductance_tiles),
+        cross, mask, place, in_hbm(conductance_tiles),
     )
 
     devices = peers * groups
-    width = 256
-    mask, place = unpack_tables(count, 24, width)
-    mask, place = jnp.asarray(mask), jnp.asarray(place)
     product, packed, held = pl.pallas_call(
         product_kernel,
         out_shape=[
@@ -441,7 +474,7 @@
             shape((devices, width // 128, 128), F32),
             pltpu.VMEM((count, rows, nodes), F32),
         ],
-        in_specs=[smem] + [vmem] * 6 + [hbm],
+        in_specs=[vmem] * 5 + [hbm],
         out_specs=[vmem] * 3,
         scratch_shapes=[
             pltpu.VMEM((width, 128), F32),
@@ -450,7 +483,7 @@
         compiler_params=params,
         cost_estimate=cost(10**9, basis_bytes),
         name="product",
-    )(nl_count, nl_nodes, returned, base, cross, mask, place, in_hbm(basis))
+    )(nl_count.reshape(1, 1), nl_nodes, returned, base, packed_gram, in_hbm(basis))
 
     gathered = lax.all_to_all(packed, DOM_HARM, 0, 0, tiled=True)
 

time: 64 us -> 62.2 us (0.972)
  Pallas kernels: 24.8 us -> 23.1 us
    pallas_call x1, Pallas kernels: 9.06 us -> 8.37 us  [local(): pl.pallas_call(vector_kernel, out_shape=[shape((rows, nodes), F32)] + [sh...]
  transfers between devices with their start and end apart: 6 -> 6, of which waited for: 0 -> 1; matrix products, arithmetic and copies ran while one was open for 0% -> 0% of each run, Pallas kernels for 11% -> 10%
where the time goes in v3:
time: 62.2 us; the launch traced here: 61.9 us
  Pallas kernels  23.1 us (37%)
  starting transfers between devices  18.8 us (30%)
  blocking collectives  18.2 us (29%)
  between operations  1.53 us (2%)
    all_to_all x1, blocking collectives, local(): gathered = lax.all_to_all(packed, DOM_HARM, 0, 0, tiled=True)  18.2 us
    pallas_call x1, Pallas kernels, local(): pl.pallas_call(vector_kernel, out_shape=[shape((rows, nodes), F32)] + [sh...  8.37 us
    all_to_all x1, starting transfers between devices, local(): arrived_spectrum = lax.all_to_all(sampled, HARM_AXES, 0, 0, tiled=True)  6.79 us
    ppermute x4, starting transfers between devices, local(): lax.ppermute(ghost, DOM, [(i, (i + jump) % peers) for i in range(peers)])  6.32 us
    all_to_all x1, starting transfers between devices, local(): returned = lax.all_to_all(leaving, HARM_AXES, 0, 0, tiled=True)  5.64 us
    pallas_call x1, Pallas kernels, local(): pl.pallas_call(coupling_kernel, out_shape=[shape((rows, nodes), F32), sha...  4.94 us
    pallas_call x1, Pallas kernels, local(): pl.pallas_call(product_kernel, out_shape=[shape((rows, nodes), F32), shap...  4.48 us
    pallas_call x1, Pallas kernels, local(): pl.pallas_call(functools.partial(residual_kernel, float(entries)), out_sh...  3.77 us
  transfers between devices with their start and end apart: 6, of which 1 were waited for; matrix products, arithmetic and copies ran while one was open for 0% of the time, Pallas kernels for 10%

profile of v3, /device:TPU:1, one launch (start us, length us, event | category | flops | bytes accessed | tf_op | source)
XLA Modules:
  0.0 61.9 jit_solution(9656036615825836499)
XLA Ops:
  0.6 0.0 copy-start.8
  0.6 0.0 copy-start
  0.7 0.0 copy-start.1
  0.7 0.0 copy-start.4
  0.7 0.0 copy-start.7
  0.7 0.0 copy-start.6
  0.7 0.0 copy-start.3
  0.7 0.0 copy-start.2
  0.7 0.0 copy-start.5
  1.4 8.4 %vector.1 = (f32[64,2048]{1,0:T(8,128)S(1)}, f32[64,128]{1,0:T(8,128)S(1)}, f32[64,128]{1,0:T(8,128)S(1)}, f32[64,128]{1,0:T(8,128)S(1)}, f32[64,128]{1,0:T(8,12...) custom-call(f32[20]{0:T(128)} %coeffs.1, s32[16]{0:T(128)} %bitcast.21, s32[1,1]{1,0:T(1,128)} %bitcast.11.nl_count, ...), custom_call_target="tpu_custom_call" | custom-call | flops 1000000000 | bytes 10485760 | tf_op jit(solution)/shard_map/vector/pallas_call | solution.py:406
  9.8 6.8 %all-to-all-start = ((f32[8,32,128]{2,1,0:T(8,128)}), f32[8,32,128]{2,1,0:T(8,128)S(1)}, u32[]{:S(2)}, u32[]{:S(2)}) async-start(f32[8,32,128]{2,1,0:T(8,128)} %get-tuple-element.16), calls=%async_computation | async-start | bytes 262144 | tf_op jit(solution)/shard_map/all_to_all | solution.py:427
  16.6 1.3 %collective-permute-start = (f32[64,128]{1,0:T(8,128)S(1)}, f32[64,128]{1,0:T(8,128)S(1)}, u32[]{:S(2)}, u32[]{:S(2)}) collective-permute-start(f32[64,128]{1,0:T(8,128)S(1)} %get-tuple-element.18), channel_id=1, source_target_pairs={{0,8},{8,16},{16,24},{24,32},{32,40},{40,48},{48,56},{56,64},{64,7... | collective-permute-start | bytes 98312 | tf_op jit(solution)/shard_map/ppermute | solution.py:429
  17.9 3.7 %collective-permute-start.1 = (f32[64,128]{1,0:T(8,128)S(1)}, f32[64,128]{1,0:T(8,128)S(1)}, u32[]{:S(2)}, u32[]{:S(2)}) collective-permute-start(f32[64,128]{1,0:T(8,128)S(1)} %get-tuple-element.19), channel_id=1, source_target_pairs={{0,120},{8,0},{16,8},{24,16},{32,24},{40,32},{48,40},{56,48},{64,5... | collective-permute-start | bytes 98312 | tf_op jit(solution)/shard_map/ppermute | solution.py:429
  21.6 1.4 %collective-permute-start.2 = (f32[64,128]{1,0:T(8,128)S(1)}, f32[64,128]{1,0:T(8,128)S(1)}, u32[]{:S(2)}, u32[]{:S(2)}) collective-permute-start(f32[64,128]{1,0:T(8,128)S(1)} %get-tuple-element.20), channel_id=1, source_target_pairs={{0,64},{8,72},{16,80},{24,88},{32,96},{40,104},{48,112},{56,120},{... | collective-permute-start | bytes 98312 | tf_op jit(solution)/shard_map/ppermute | solution.py:429
  22.9 0.0 collective-permute-start.3
  22.9 0.0 all-to-all-done.arrived
  22.9 0.0 copy-done.8
  22.9 0.0 copy-done.7
  23.0 0.0 copy-done.6
  23.0 1.5 %current.1 = f32[8,32,128]{2,1,0:T(8,128)} custom-call(f32[8,32,128]{2,1,0:T(8,128)S(1)} %all-to-all-done.arrived, f32[64,512]{1,0:T(8,128)S(1)} %bitcast.16, f32[1,64]{1,0:T(1,128)S(1)} %bitcast.17, bf16[6,256,256]{2,1,0:T(8,128)(2,1)S(1)} %copy-done.8), custom_call_target="tpu_custom_call" | custom-call | flops 400000000 | bytes 2000000 | tf_op jit(solution)/shard_map/current/pallas_call | solution.py:433
  24.5 5.6 %all-to-all-start.1 = ((f32[8,32,128]{2,1,0:T(8,128)}), f32[8,32,128]{2,1,0:T(8,128)S(1)}, u32[]{:S(2)}, u32[]{:S(2)}) async-start(f32[8,32,128]{2,1,0:T(8,128)} %current.1), calls=%async_computation.1 | async-start | bytes 262144 | tf_op jit(solution)/shard_map/all_to_all | solution.py:443
  30.1 0.0 collective-permute-done.ghost_0
  30.1 0.0 collective-permute-done.1.ghost_1
  30.1 0.0 collective-permute-done.2.ghost_2
  30.2 0.0 collective-permute-done.3.ghost_3
  30.2 0.0 copy-done
  30.2 0.0 copy-done.1
  30.2 0.0 copy-done.3
  30.2 0.0 copy-done.2
  30.2 0.0 copy-done.5
  30.2 4.9 %coupling.1 = (f32[64,2048]{1,0:T(8,128)S(1)}, f32[1,256]{1,0:T(1,128)S(1)}) custom-call(s32[6,16]{1,0:T(8,128)S(1)} %bitcast.15, f32[64,2048]{1,0:T(8,128)S(1)} %get-tuple-element.17.vector, f32[64,128]{1,0:T(8,128)S(1)} %collective-permute-done.ghost_0, f32[64,128]{1,0:T(8,128)S(1)} %collective-permute-done.1.ghost_1, ...), custom_call_target="tpu_custom_call" | custom-call | flops 1000000000 | bytes 6291456 | tf_op jit(solution)/shard_map/coupling/pallas_call | solution.py:449
  35.2 0.2 all-to-all-done.1.arrived
  35.4 0.0 copy-done.4
  35.4 4.5 %product.1 = (f32[64,2048]{1,0:T(8,128)S(1)}, f32[128,2,128]{2,1,0:T(2,128)S(1)}, f32[20,64,2048]{2,1,0:T(8,128)S(1)}) custom-call(s32[1,1]{1,0:T(1,128)} %bitcast.12.nl_count, s32[1,512]{1,0:T(1,128)S(1)} %copy-done.4, f32[8,32,128]{2,1,0:T(8,128)S(1)} %all-to-all-done.1.arrived, f32[64,2048]{1,0:T(8,128)S(1)} %get-tuple-element.23.base, ...), custom_call_target="tpu_custom_call" | custom-call | flops 1000000000 | bytes 10485760 | tf_op jit(solution)/shard_map/product/pallas_call | solution.py:470
  39.9 18.2 %all_to_all.15.gathered = f32[128,2,128]{2,1,0:T(2,128)S(1)} all-to-all(f32[128,2,128]{2,1,0:T(2,128)S(1)} %get-tuple-element.25), channel_id=1, replica_groups=mesh['dom_0'=4,'dom_1'=4,'harm_0'=4,'harm_1'=2] {'dom_0','dom_1','harm_0..., dimensions={0} | all-to-all | bytes 262144 | tf_op jit(solution)/shard_map/all_to_all | solution.py:488
  58.1 3.8 %residual.1 = (f32[64,2048]{1,0:T(8,128)}, f32[1,21]{1,0:T(1,128)}) custom-call(f32[128,2,128]{2,1,0:T(2,128)S(1)} %all_to_all.15.gathered, f32[2,24,256]{2,1,0:T(8,128)S(1)} %copy-done.1, bf16[2,256,128]{2,1,0:T(8,128)(2,1)S(1)} %copy-done, f32[64,2048]{1,0:T(8,128)S(1)} %get-tuple-element.26.product, f32[20,64,2048]{2,1,0:T(8,128)S(1)} %get-tuple-element.27.basis), custom_call_target="tpu_custom_call" | custom-call | flops 1000000000 | bytes 10485760 | tf_op jit(solution)/shard_map/residual/pallas_call | solution.py:491
Async XLA Ops:
  0.6 22.3 %copy-start.8 = (bf16[6,256,256]{2,1,0:T(8,128)(2,1)S(1)}, bf16[6,256,256]{2,1,0:T(8,128)(2,1)}, u32[]{:S(2)}) copy-start(bf16[6,256,256]{2,1,0:T(8,128)(2,1)} %constant.6.clone.tables) | copy-start | bytes 2359300
  0.6 29.5 %copy-start = (bf16[2,256,128]{2,1,0:T(8,128)(2,1)S(1)}, bf16[2,256,128]{2,1,0:T(8,128)(2,1)}, u32[]{:S(2)}) copy-start(bf16[2,256,128]{2,1,0:T(8,128)(2,1)} %constant.8.clone.place) | copy-start | bytes 393220
  0.7 29.5 %copy-start.1 = (f32[2,24,256]{2,1,0:T(8,128)S(1)}, f32[2,24,256]{2,1,0:T(8,128)}, u32[]{:S(2)}) copy-start(f32[2,24,256]{2,1,0:T(8,128)} %constant.7.clone.mask) | copy-start | bytes 147460
  0.7 34.7 %copy-start.4 = (s32[1,512]{1,0:T(1,128)S(1)}, s32[1,512]{1,0:T(1,128)}, u32[]{:S(2)}) copy-start(s32[1,512]{1,0:T(1,128)} %nl_nodes.3) | copy-start | bytes 6148
  0.7 22.3 %copy-start.7 = (f32[64]{0:T(128)S(1)}, f32[64]{0:T(128)}, u32[]{:S(2)}) copy-start(f32[64]{0:T(128)} %param.26) | copy-start | bytes 772
  0.7 22.3 %copy-start.6 = (f32[512,64]{0,1:T(8,128)S(1)}, f32[512,64]{0,1:T(8,128)}, u32[]{:S(2)}) copy-start(f32[512,64]{0,1:T(8,128)} %param.25) | copy-start | bytes 393220
  0.7 29.5 %copy-start.3 = (f32[2048]{0:T(1024)S(1)}, f32[2048]{0:T(1024)}, u32[]{:S(2)}) copy-start(f32[2048]{0:T(1024)} %param.20) | copy-start | bytes 24580
  0.7 29.5 %copy-start.2 = (f32[2048]{0:T(1024)S(1)}, f32[2048]{0:T(1024)}, u32[]{:S(2)}) copy-start(f32[2048]{0:T(1024)} %param.19) | copy-start | bytes 24580
  0.7 29.5 %copy-start.5 = (s32[16,6]{0,1:T(8,128)S(1)}, s32[16,6]{0,1:T(8,128)}, u32[]{:S(2)}) copy-start(s32[16,6]{0,1:T(8,128)} %param.18) | copy-start | bytes 1156
  9.8 13.1 %all-to-all-start = ((f32[8,32,128]{2,1,0:T(8,128)}), f32[8,32,128]{2,1,0:T(8,128)S(1)}, u32[]{:S(2)}, u32[]{:S(2)}) async-start(f32[8,32,128]{2,1,0:T(8,128)} %get-tuple-element.16), calls=%async_computation | async-start | bytes 262144 | tf_op jit(solution)/shard_map/all_to_all | solution.py:427
  16.6 13.5 %collective-permute-start = (f32[64,128]{1,0:T(8,128)S(1)}, f32[64,128]{1,0:T(8,128)S(1)}, u32[]{:S(2)}, u32[]{:S(2)}) collective-permute-start(f32[64,128]{1,0:T(8,128)S(1)} %get-tuple-element.18), channel_id=1, source_target_pairs={{0,8},{8,16},{16,24},{24,32},{32,40},{40,48},{48,56},{56,64},{64,7... | collective-permute-start | bytes 98312 | tf_op jit(solution)/shard_map/ppermute | solution.py:429
  17.9 12.2 %collective-permute-start.1 = (f32[64,128]{1,0:T(8,128)S(1)}, f32[64,128]{1,0:T(8,128)S(1)}, u32[]{:S(2)}, u32[]{:S(2)}) collective-permute-start(f32[64,128]{1,0:T(8,128)S(1)} %get-tuple-element.19), channel_id=1, source_target_pairs={{0,120},{8,0},{16,8},{24,16},{32,24},{40,32},{48,40},{56,48},{64,5... | collective-permute-start | bytes 98312 | tf_op jit(solution)/shard_map/ppermute | solution.py:429
  21.6 8.6 %collective-permute-start.2 = (f32[64,128]{1,0:T(8,128)S(1)}, f32[64,128]{1,0:T(8,128)S(1)}, u32[]{:S(2)}, u32[]{:S(2)}) collective-permute-start(f32[64,128]{1,0:T(8,128)S(1)} %get-tuple-element.20), channel_id=1, source_target_pairs={{0,64},{8,72},{16,80},{24,88},{32,96},{40,104},{48,112},{56,120},{... | collective-permute-start | bytes 98312 | tf_op jit(solution)/shard_map/ppermute | solution.py:429
  22.9 7.2 %collective-permute-start.3 = (f32[64,128]{1,0:T(8,128)S(1)}, f32[64,128]{1,0:T(8,128)S(1)}, u32[]{:S(2)}, u32[]{:S(2)}) collective-permute-start(f32[64,128]{1,0:T(8,128)S(1)} %get-tuple-element.21), channel_id=1, source_target_pairs={{0,72},{8,80},{16,88},{24,96},{32,104},{40,112},{48,120},{56,0},{6... | collective-permute-start | bytes 98312 | tf_op jit(solution)/shard_map/ppermute | solution.py:429
  24.5 10.9 %all-to-all-start.1 = ((f32[8,32,128]{2,1,0:T(8,128)}), f32[8,32,128]{2,1,0:T(8,128)S(1)}, u32[]{:S(2)}, u32[]{:S(2)}) async-start(f32[8,32,128]{2,1,0:T(8,128)} %current.1), calls=%async_computation.1 | async-start | bytes 262144 | tf_op jit(solution)/shard_map/all_to_all | solution.py:443

commit v4 on v3

--- a/solution.py
+++ b/solution.py
@@ -93,7 +93,7 @@
     return sum(mm_nt(ones, part) for part in thirds(rows_ref[...]))
 
 
-def vector_kernel(coeffs, send_count, nl_count, send_nodes, nl_nodes, basis_hbm,
+def vector_kernel(coeffs, send_count, send_nodes, nl_nodes, basis_hbm,
                   vector, ghost_0, ghost_1, ghost_2, ghost_3, sampled, cross,
                   basis, select, sems):
     start_all(basis_hbm, basis, sems)
@@ -108,8 +108,7 @@
         peer = lax.rem(me + step, peers)
         listed = send_nodes[pl.ds(peer, 1), :]
         wanted.append(jnp.where(lane < send_count[peer], listed, -1))
-    slot = lax.broadcasted_iota(jnp.int32, (1, slots), 1)
-    wanted.append(jnp.where(slot < nl_count[...], nl_nodes[...], -1))
+    wanted.append(nl_nodes[...])
     columns = jnp.concatenate(wanted, axis=1)
     cross[...] = jnp.zeros_like(cross)
 
@@ -279,7 +278,7 @@
     half = rows // 2
     slots = nl_nodes.shape[1]
     slot = lax.broadcasted_iota(jnp.int32, (1, slots), 1)
-    columns = jnp.where(slot < nl_count[...], nl_nodes[...], -1)
+    columns = jnp.where(slot < nl_count[0], nl_nodes[...], -1)
     low_lanes = lax.broadcasted_iota(jnp.int32, (half, 128), 1) < 64
     top, bottom = [], []
     for pair in range(slots // 128):
@@ -409,7 +408,7 @@
         + [shape((rows, peer_cap), F32)] * len(PEERS)
         + [shape((groups, harm_local, 128), F32)]
         + [shape((count * 16, count * 8), F32)],
-        in_specs=[smem, smem, vmem, vmem, vmem, hbm],
+        in_specs=[smem, smem, vmem, vmem, hbm],
         out_specs=[vmem] * (3 + len(PEERS)),
         scratch_shapes=[
             pltpu.VMEM((count, rows, nodes), F32),
@@ -420,7 +419,7 @@
         cost_estimate=cost(10**9, basis_bytes),
         name="vector",
     )(
-        in_hbm(coeffs), in_hbm(send_count[0]), nl_count.reshape(1, 1),
+        in_hbm(coeffs), in_hbm(send_count[0]),
         in_hbm(send_nodes[0]), in_hbm(nl_nodes), in_hbm(basis),
     )
 
@@ -474,7 +473,7 @@
             shape((devices, width // 128, 128), F32),
             pltpu.VMEM((count, rows, nodes), F32),
         ],
-        in_specs=[vmem] * 5 + [hbm],
+        in_specs=[smem] + [vmem] * 4 + [hbm],
         out_specs=[vmem] * 3,
         scratch_shapes=[
             pltpu.VMEM((width, 128), F32),
@@ -483,7 +482,7 @@
         compiler_params=params,
         cost_estimate=cost(10**9, basis_bytes),
         name="product",
-    )(nl_count.reshape(1, 1), nl_nodes, returned, base, packed_gram, in_hbm(basis))
+    )(nl_count, nl_nodes, returned, base, packed_gram, in_hbm(basis))
 
     gathered = lax.all_to_all(packed, DOM_HARM, 0, 0, tiled=True)
 

time: 62.2 us -> 62.3 us (level)
  transfers between devices with their start and end apart: 6 -> 6, of which waited for: 1 -> 0; matrix products, arithmetic and copies ran while one was open for 0% -> 0% of each run, Pallas kernels for 10% -> 10%
where the time goes in v4:
time: 62.3 us; the launch traced here: 61.9 us
  Pallas kernels  23.2 us (37%)
  starting transfers between devices  18.7 us (30%)
  blocking collectives  18.4 us (30%)
  between operations  1.49 us (2%)
    all_to_all x1, blocking collectives, local(): gathered = lax.all_to_all(packed, DOM_HARM, 0, 0, tiled=True)  18.4 us
    pallas_call x1, Pallas kernels, local(): pl.pallas_call(vector_kernel, out_shape=[shape((rows, nodes), F32)] + [sh...  8.48 us
    all_to_all x1, starting transfers between devices, local(): arrived_spectrum = lax.all_to_all(sampled, HARM_AXES, 0, 0, tiled=True)  6.77 us
    ppermute x4, starting transfers between devices, local(): lax.ppermute(ghost, DOM, [(i, (i + jump) % peers) for i in range(peers)])  6.32 us
    all_to_all x1, starting transfers between devices, local(): returned = lax.all_to_all(leaving, HARM_AXES, 0, 0, tiled=True)  5.64 us
    pallas_call x1, Pallas kernels, local(): pl.pallas_call(coupling_kernel, out_shape=[shape((rows, nodes), F32), sha...  4.94 us
    pallas_call x1, Pallas kernels, local(): pl.pallas_call(product_kernel, out_shape=[shape((rows, nodes), F32), shap...  4.45 us
    pallas_call x1, Pallas kernels, local(): pl.pallas_call(functools.partial(residual_kernel, float(entries)), out_sh...  3.77 us
  transfers between devices with their start and end apart: 6, of which 0 were waited for; matrix products, arithmetic and copies ran while one was open for 0% of the time, Pallas kernels for 10%

profile of v4, /device:TPU:1, one launch (start us, length us, event | category | flops | bytes accessed | tf_op | source)
XLA Modules:
  0.0 61.9 jit_solution(6975944889481875928)
XLA Ops:
  0.6 0.0 copy-start.8
  0.6 0.0 copy-start
  0.7 0.0 copy-start.1
  0.7 0.0 copy-start.4
  0.7 0.0 copy-start.7
  0.7 0.0 copy-start.6
  0.7 0.0 copy-start.3
  0.7 0.0 copy-start.2
  0.7 0.0 copy-start.5
  0.7 8.5 %vector.1 = (f32[64,2048]{1,0:T(8,128)S(1)}, f32[64,128]{1,0:T(8,128)S(1)}, f32[64,128]{1,0:T(8,128)S(1)}, f32[64,128]{1,0:T(8,128)S(1)}, f32[64,128]{1,0:T(8,12...) custom-call(f32[20]{0:T(128)} %coeffs.1, s32[16]{0:T(128)} %bitcast.18, s32[16,128]{1,0:T(8,128)} %bitcast.17, ...), custom_call_target="tpu_custom_call" | custom-call | flops 1000000000 | bytes 10485760 | tf_op jit(solution)/shard_map/vector/pallas_call | solution.py:405
  9.2 6.8 %all-to-all-start = ((f32[8,32,128]{2,1,0:T(8,128)}), f32[8,32,128]{2,1,0:T(8,128)S(1)}, u32[]{:S(2)}, u32[]{:S(2)}) async-start(f32[8,32,128]{2,1,0:T(8,128)} %get-tuple-element.16), calls=%async_computation | async-start | bytes 262144 | tf_op jit(solution)/shard_map/all_to_all | solution.py:426
  16.0 1.4 %collective-permute-start = (f32[64,128]{1,0:T(8,128)S(1)}, f32[64,128]{1,0:T(8,128)S(1)}, u32[]{:S(2)}, u32[]{:S(2)}) collective-permute-start(f32[64,128]{1,0:T(8,128)S(1)} %get-tuple-element.18), channel_id=1, source_target_pairs={{0,8},{8,16},{16,24},{24,32},{32,40},{40,48},{48,56},{56,64},{64,7... | collective-permute-start | bytes 98312 | tf_op jit(solution)/shard_map/ppermute | solution.py:428
  17.3 3.6 %collective-permute-start.1 = (f32[64,128]{1,0:T(8,128)S(1)}, f32[64,128]{1,0:T(8,128)S(1)}, u32[]{:S(2)}, u32[]{:S(2)}) collective-permute-start(f32[64,128]{1,0:T(8,128)S(1)} %get-tuple-element.19), channel_id=1, source_target_pairs={{0,120},{8,0},{16,8},{24,16},{32,24},{40,32},{48,40},{56,48},{64,5... | collective-permute-start | bytes 98312 | tf_op jit(solution)/shard_map/ppermute | solution.py:428
  20.9 1.4 %collective-permute-start.2 = (f32[64,128]{1,0:T(8,128)S(1)}, f32[64,128]{1,0:T(8,128)S(1)}, u32[]{:S(2)}, u32[]{:S(2)}) collective-permute-start(f32[64,128]{1,0:T(8,128)S(1)} %get-tuple-element.20), channel_id=1, source_target_pairs={{0,64},{8,72},{16,80},{24,88},{32,96},{40,104},{48,112},{56,120},{... | collective-permute-start | bytes 98312 | tf_op jit(solution)/shard_map/ppermute | solution.py:428
  22.3 0.0 collective-permute-start.3
  22.3 0.0 all-to-all-done.arrived
  22.3 0.0 copy-done.8
  22.3 0.0 copy-done.7
  22.3 0.0 copy-done.6
  22.3 1.5 %current.1 = f32[8,32,128]{2,1,0:T(8,128)} custom-call(f32[8,32,128]{2,1,0:T(8,128)S(1)} %all-to-all-done.arrived, f32[64,512]{1,0:T(8,128)S(1)} %bitcast.13, f32[1,64]{1,0:T(1,128)S(1)} %bitcast.14, bf16[6,256,256]{2,1,0:T(8,128)(2,1)S(1)} %copy-done.8), custom_call_target="tpu_custom_call" | custom-call | flops 400000000 | bytes 2000000 | tf_op jit(solution)/shard_map/current/pallas_call | solution.py:432
  23.9 5.6 %all-to-all-start.1 = ((f32[8,32,128]{2,1,0:T(8,128)}), f32[8,32,128]{2,1,0:T(8,128)S(1)}, u32[]{:S(2)}, u32[]{:S(2)}) async-start(f32[8,32,128]{2,1,0:T(8,128)} %current.1), calls=%async_computation.1 | async-start | bytes 262144 | tf_op jit(solution)/shard_map/all_to_all | solution.py:442
  30.2 0.0 collective-permute-done.ghost_0
  30.2 0.0 collective-permute-done.1.ghost_1
  30.2 0.0 collective-permute-done.2.ghost_2
  30.2 0.0 collective-permute-done.3.ghost_3
  30.2 0.0 copy-done
  30.2 0.0 copy-done.1
  30.2 0.0 copy-done.3
  30.2 0.0 copy-done.2
  30.2 0.0 copy-done.5
  30.2 4.9 %coupling.1 = (f32[64,2048]{1,0:T(8,128)S(1)}, f32[1,256]{1,0:T(1,128)S(1)}) custom-call(s32[6,16]{1,0:T(8,128)S(1)} %bitcast.12, f32[64,2048]{1,0:T(8,128)S(1)} %get-tuple-element.17.vector, f32[64,128]{1,0:T(8,128)S(1)} %collective-permute-done.ghost_0, f32[64,128]{1,0:T(8,128)S(1)} %collective-permute-done.1.ghost_1, ...), custom_call_target="tpu_custom_call" | custom-call | flops 1000000000 | bytes 6291456 | tf_op jit(solution)/shard_map/coupling/pallas_call | solution.py:448
  35.2 0.0 all-to-all-done.1.arrived
  35.2 0.0 copy-done.4
  35.2 4.5 %product.1 = (f32[64,2048]{1,0:T(8,128)S(1)}, f32[128,2,128]{2,1,0:T(2,128)S(1)}, f32[20,64,2048]{2,1,0:T(8,128)S(1)}) custom-call(s32[1]{0:T(128)S(6)} %copy.17.nl_count, s32[1,512]{1,0:T(1,128)S(1)} %copy-done.4, f32[8,32,128]{2,1,0:T(8,128)S(1)} %all-to-all-done.1.arrived, f32[64,2048]{1,0:T(8,128)S(1)} %get-tuple-element.23.base, ...), custom_call_target="tpu_custom_call" | custom-call | flops 1000000000 | bytes 10485760 | tf_op jit(solution)/shard_map/product/pallas_call | solution.py:469
  39.7 18.4 %all_to_all.15.gathered = f32[128,2,128]{2,1,0:T(2,128)S(1)} all-to-all(f32[128,2,128]{2,1,0:T(2,128)S(1)} %get-tuple-element.25), channel_id=1, replica_groups=mesh['dom_0'=4,'dom_1'=4,'harm_0'=4,'harm_1'=2] {'dom_0','dom_1','harm_0..., dimensions={0} | all-to-all | bytes 262144 | tf_op jit(solution)/shard_map/all_to_all | solution.py:487
  58.1 3.8 %residual.1 = (f32[64,2048]{1,0:T(8,128)}, f32[1,21]{1,0:T(1,128)}) custom-call(f32[128,2,128]{2,1,0:T(2,128)S(1)} %all_to_all.15.gathered, f32[2,24,256]{2,1,0:T(8,128)S(1)} %copy-done.1, bf16[2,256,128]{2,1,0:T(8,128)(2,1)S(1)} %copy-done, f32[64,2048]{1,0:T(8,128)S(1)} %get-tuple-element.26.product, f32[20,64,2048]{2,1,0:T(8,128)S(1)} %get-tuple-element.27.basis), custom_call_target="tpu_custom_call" | custom-call | flops 1000000000 | bytes 10485760 | tf_op jit(solution)/shard_map/residual/pallas_call | solution.py:490
Async XLA Ops:
  0.6 21.7 %copy-start.8 = (bf16[6,256,256]{2,1,0:T(8,128)(2,1)S(1)}, bf16[6,256,256]{2,1,0:T(8,128)(2,1)}, u32[]{:S(2)}) copy-start(bf16[6,256,256]{2,1,0:T(8,128)(2,1)} %constant.6.clone.tables) | copy-start | bytes 2359300
  0.6 29.6 %copy-start = (bf16[2,256,128]{2,1,0:T(8,128)(2,1)S(1)}, bf16[2,256,128]{2,1,0:T(8,128)(2,1)}, u32[]{:S(2)}) copy-start(bf16[2,256,128]{2,1,0:T(8,128)(2,1)} %constant.8.clone.place) | copy-start | bytes 393220
  0.7 29.5 %copy-start.1 = (f32[2,24,256]{2,1,0:T(8,128)S(1)}, f32[2,24,256]{2,1,0:T(8,128)}, u32[]{:S(2)}) copy-start(f32[2,24,256]{2,1,0:T(8,128)} %constant.7.clone.mask) | copy-start | bytes 147460
  0.7 34.5 %copy-start.4 = (s32[1,512]{1,0:T(1,128)S(1)}, s32[1,512]{1,0:T(1,128)}, u32[]{:S(2)}) copy-start(s32[1,512]{1,0:T(1,128)} %nl_nodes.3) | copy-start | bytes 6148
  0.7 21.6 %copy-start.7 = (f32[64]{0:T(128)S(1)}, f32[64]{0:T(128)}, u32[]{:S(2)}) copy-start(f32[64]{0:T(128)} %param.26) | copy-start | bytes 772
  0.7 21.6 %copy-start.6 = (f32[512,64]{0,1:T(8,128)S(1)}, f32[512,64]{0,1:T(8,128)}, u32[]{:S(2)}) copy-start(f32[512,64]{0,1:T(8,128)} %param.25) | copy-start | bytes 393220
  0.7 29.5 %copy-start.3 = (f32[2048]{0:T(1024)S(1)}, f32[2048]{0:T(1024)}, u32[]{:S(2)}) copy-start(f32[2048]{0:T(1024)} %param.20) | copy-start | bytes 24580
  0.7 29.5 %copy-start.2 = (f32[2048]{0:T(1024)S(1)}, f32[2048]{0:T(1024)}, u32[]{:S(2)}) copy-start(f32[2048]{0:T(1024)} %param.19) | copy-start | bytes 24580
  0.7 29.5 %copy-start.5 = (s32[16,6]{0,1:T(8,128)S(1)}, s32[16,6]{0,1:T(8,128)}, u32[]{:S(2)}) copy-start(s32[16,6]{0,1:T(8,128)} %param.18) | copy-start | bytes 1156
  9.2 13.1 %all-to-all-start = ((f32[8,32,128]{2,1,0:T(8,128)}), f32[8,32,128]{2,1,0:T(8,128)S(1)}, u32[]{:S(2)}, u32[]{:S(2)}) async-start(f32[8,32,128]{2,1,0:T(8,128)} %get-tuple-element.16), calls=%async_computation | async-start | bytes 262144 | tf_op jit(solution)/shard_map/all_to_all | solution.py:426
  16.0 14.2 %collective-permute-start = (f32[64,128]{1,0:T(8,128)S(1)}, f32[64,128]{1,0:T(8,128)S(1)}, u32[]{:S(2)}, u32[]{:S(2)}) collective-permute-start(f32[64,128]{1,0:T(8,128)S(1)} %get-tuple-element.18), channel_id=1, source_target_pairs={{0,8},{8,16},{16,24},{24,32},{32,40},{40,48},{48,56},{56,64},{64,7... | collective-permute-start | bytes 98312 | tf_op jit(solution)/shard_map/ppermute | solution.py:428
  17.3 12.8 %collective-permute-start.1 = (f32[64,128]{1,0:T(8,128)S(1)}, f32[64,128]{1,0:T(8,128)S(1)}, u32[]{:S(2)}, u32[]{:S(2)}) collective-permute-start(f32[64,128]{1,0:T(8,128)S(1)} %get-tuple-element.19), channel_id=1, source_target_pairs={{0,120},{8,0},{16,8},{24,16},{32,24},{40,32},{48,40},{56,48},{64,5... | collective-permute-start | bytes 98312 | tf_op jit(solution)/shard_map/ppermute | solution.py:428
  20.9 9.2 %collective-permute-start.2 = (f32[64,128]{1,0:T(8,128)S(1)}, f32[64,128]{1,0:T(8,128)S(1)}, u32[]{:S(2)}, u32[]{:S(2)}) collective-permute-start(f32[64,128]{1,0:T(8,128)S(1)} %get-tuple-element.20), channel_id=1, source_target_pairs={{0,64},{8,72},{16,80},{24,88},{32,96},{40,104},{48,112},{56,120},{... | collective-permute-start | bytes 98312 | tf_op jit(solution)/shard_map/ppermute | solution.py:428
  22.3 7.9 %collective-permute-start.3 = (f32[64,128]{1,0:T(8,128)S(1)}, f32[64,128]{1,0:T(8,128)S(1)}, u32[]{:S(2)}, u32[]{:S(2)}) collective-permute-start(f32[64,128]{1,0:T(8,128)S(1)} %get-tuple-element.21), channel_id=1, source_target_pairs={{0,72},{8,80},{16,88},{24,96},{32,104},{40,112},{48,120},{56,0},{6... | collective-permute-start | bytes 98312 | tf_op jit(solution)/shard_map/ppermute | solution.py:428
  23.9 11.3 %all-to-all-start.1 = ((f32[8,32,128]{2,1,0:T(8,128)}), f32[8,32,128]{2,1,0:T(8,128)S(1)}, u32[]{:S(2)}, u32[]{:S(2)}) async-start(f32[8,32,128]{2,1,0:T(8,128)} %current.1), calls=%async_computation.1 | async-start | bytes 262144 | tf_op jit(solution)/shard_map/all_to_all | solution.py:442
